TPU v7x, 128 devices: a whole 4x4x4 slice. The times are simulated.
128 devices in a mesh: io: 64 (over z, x, y_lo, core), rep: 2 (over y_hi).
Axes of the slice: x: 4, y: 4 (y_hi: 2, y_lo: 2; y = y_hi * 2 + y_lo), z: 4, core: 2. Of those that a mesh axis runs over, the one named last changes fastest.
Arguments:
- snapshots: float32 [49152, 8192], P(('rep', 'io')), parts along dimension 0, may hold values from -6 to 6
Outputs:
- coefficients: float32 [32, 256, 8192], P('rep', None, 'io'), parts along dimension 0
- resid_var: float32 [512, 8192], P('rep', 'io'), parts along dimension 0
There are 2 independent parts, one for each index of `rep`. A program takes and returns all parts, laid end to end along the dimension named above; each array names one. Nothing has to cross between parts.
All inputs are finite; a program needn't handle non-finite values.
Results may differ from a plain program's by a relative error of at most 0.000071.
Values sent between devices are 32-bit elements; how exact they have to be, the bound alone decides.
A program may use at most 128 MiB of HBM per device.

v0:
```python
import jax
import jax.numpy as jnp
from jax import lax
from jax.sharding import PartitionSpec as P

TIMES = 96
HARM = 16


def basis_matrix(times):
    steps = jnp.arange(times).astype(jnp.float32)
    columns = [jnp.ones_like(steps), (steps - (times - 1) / 2.0) / (times / 2.0)]
    for harmonic in range(1, 7):
        columns.append(jnp.cos(2.0 * jnp.pi * harmonic * steps / 12.0))
    for harmonic in range(1, 6):
        columns.append(jnp.sin(2.0 * jnp.pi * harmonic * steps / 12.0))
    columns.append(jnp.cos(2.0 * jnp.pi * steps / times))
    columns.append(jnp.sin(2.0 * jnp.pi * steps / times))
    columns.append(jnp.cos(4.0 * jnp.pi * steps / times))
    return jnp.stack(columns, axis=1)


def projector_of(basis):
    gram = jnp.dot(basis.T, basis, precision=lax.Precision.HIGHEST)
    factor = jnp.linalg.cholesky(gram)
    middle = lax.linalg.triangular_solve(factor, basis.T, left_side=True, lower=True)
    return lax.linalg.triangular_solve(factor, middle, left_side=True, lower=True, transpose_a=True)


def fit_block(block, basis, projector):
    width = block.shape[-1]
    lat_rows = block.shape[0] // TIMES
    series = block.reshape(TIMES, lat_rows * width)
    coeffs = jnp.dot(projector, series, precision=lax.Precision.HIGHEST)
    moments = jnp.dot(basis.T, series, precision=lax.Precision.HIGHEST)
    total = jnp.sum(series * series, axis=0)
    variance = (total - jnp.sum(coeffs * moments, axis=0)) / TIMES
    return (coeffs.reshape(HARM, lat_rows, width), variance.reshape(1, lat_rows, width))


def local(snapshots):
    groups = lax.axis_size("io")
    local_rows = snapshots.shape[0]
    lon_dev = snapshots.shape[1] // groups
    split_view = snapshots.reshape(local_rows, groups, lon_dev)
    basis = basis_matrix(TIMES)
    projector = projector_of(basis)
    moved = lax.all_to_all(split_view, "io", split_axis=1, concat_axis=0, tiled=True)
    coeffs, variance = fit_block(moved[:, 0, :], basis, projector)
    return (coeffs, variance[0])


def solution(mesh):
    placed = (P(("rep", "io"), None),)
    return jax.shard_map(
        local,
        mesh=mesh,
        in_specs=placed,
        out_specs=(P("rep", None, "io"), P("rep", "io")),
        check_vma=False,
    )
```

profile of v0, /device:TPU:1, one launch (start us, length us, event | category | flops | bytes accessed | tf_op | source)
XLA Modules:
  0.0 227.6 jit_solution(6432960460705111919)
XLA Ops:
  0.6 10.7 %copy_bitcast_fusion = f32[384,64,128]{2,0,1:T(8,128)} fusion(f32[384,8192]{1,0:T(8,128)} %param.1), kind=kLoop, calls=%fused_computation.1 | loop fusion | bytes 25165824 | tf_op jit(solution)/shard_map/reshape | solution.py:45
  11.4 11.0 %all-to-all-start = ((f32[384,64,128]{2,0,1:T(8,128)}), f32[384,64,128]{2,0,1:T(8,128)}, u32[]{:S(2)}, u32[]{:S(2)}) async-start(f32[384,64,128]{2,0,1:T(8,128)} %copy_bitcast_fusion), calls=%async_computation | async-start | bytes 25165824 | tf_op jit(solution)/shard_map/all_to_all | solution.py:48
  22.4 0.1 fusion.16
  22.5 0.1 fusion.14
  22.5 0.1 fusion.12
  22.6 0.1 fusion.10
  22.6 0.1 fusion.8
  22.7 0.1 multiply_cosine_fusion
  22.8 0.1 stack.2
  22.9 0.1 fusion.19
  23.0 0.1 copy.6
  23.1 1.5 cholesky.16
  24.6 0.6 compare_reduce_fusion
  25.2 0.6 fusion.1
  25.9 1.2 custom-call.8
  27.1 0.2 fusion.4
  27.3 0.1 fusion.2
  27.4 163.7 %all-to-all-done = f32[384,64,128]{2,0,1:T(8,128)} async-done(((f32[384,64,128]{2,0,1:T(8,128)}), f32[384,64,128]{2,0,1:T(8,128)}, u32[]{:S(2)}, u32[]{:S(2)}) %all-to-all-start) | async-done | bytes 12582944 | tf_op jit(solution)/shard_map/all_to_all | solution.py:48
  191.2 13.8 %reshape_squeeze.3 = f32[96,32768]{1,0:T(8,128)} reshape(f32[64,384,1,128]{3,1,0,2:T(8,128)} %bitcast.4) | data formatting | bytes 25165824 | tf_op jit(solution)/shard_map/reshape;squeeze | solution.py:33
  205.0 0.0 copy-start
  205.0 5.8 %multiply_reduce_fusion = f32[32768]{0:T(1024)S(1)} fusion(f32[96,32768]{1,0:T(8,128)} %reshape_squeeze.3), kind=kLoop, calls=%fused_computation.2 | loop fusion | flops 6258688 | bytes 12713984 | tf_op jit(solution)/shard_map/reduce_sum | solution.py:36
  210.8 2.4 %copy-done = f32[96,32768]{1,0:T(8,128)S(1)} copy-done((f32[96,32768]{1,0:T(8,128)S(1)}, f32[96,32768]{1,0:T(8,128)}, u32[]{:S(2)}) %copy-start) | copy-done | bytes 12582936
  213.1 6.0 %fusion.20 = f32[16,32768]{1,0:T(8,128)S(1)} fusion(f32[16,96]{1,0:T(8,128)S(1)} %fusion.2, f32[96,32768]{1,0:T(8,128)S(1)} %copy-done), kind=kOutput, calls=%fused_computation.39 | convolution fusion | flops 603979776 | bytes 14686208 | tf_op jit(solution)/shard_map/dot_general | solution.py:34
  219.1 6.1 %fusion = f32[32768]{0:T(1024)S(1)} fusion(f32[16,32768]{1,0:T(8,128)S(1)} %fusion.20, f32[96,16]{0,1:T(8,128)S(1)} %stack.2, f32[96,32768]{1,0:T(8,128)S(1)} %copy-done), kind=kOutput, calls=%fused_computation.3 | convolution fusion | flops 604995584 | bytes 14817280 | tf_op jit(solution)/shard_map/dot_general | solution.py:35
  225.2 1.7 copy.9
  226.9 0.7 multiply_bitcast_fusion
  (5 shorter events, 0.1 us)
Async XLA Ops:
  11.4 179.8 %all-to-all-start = ((f32[384,64,128]{2,0,1:T(8,128)}), f32[384,64,128]{2,0,1:T(8,128)}, u32[]{:S(2)}, u32[]{:S(2)}) async-start(f32[384,64,128]{2,0,1:T(8,128)} %copy_bitcast_fusion), calls=%async_computation | async-start | bytes 25165824 | tf_op jit(solution)/shard_map/all_to_all | solution.py:48
  205.0 8.2 %copy-start = (f32[96,32768]{1,0:T(8,128)S(1)}, f32[96,32768]{1,0:T(8,128)}, u32[]{:S(2)}) copy-start(f32[96,32768]{1,0:T(8,128)} %reshape_squeeze.3) | copy-start | bytes 37748740
where the time goes:
time: 229 us; the launch traced here: 228 us
  waiting for transfers between devices  164 us (72%)
  local copies, waits for them, and re-layouts  28.8 us (13%)
  matrix products  12.5 us (5%)
  starting transfers between devices  11 us (5%)
  other arithmetic  10.9 us (5%)
    all_to_all x1, waiting for transfers between devices, local(): lax.all_to_all(split_view, 'io', split_axis=1, concat_axis=0, tiled=True)  164 us
    another operation x1, local copies, waits for them, and re-layouts, fit_block(): series = block.reshape(TIMES, lat_rows * width)  13.8 us
    all_to_all x1, starting transfers between devices, local(): lax.all_to_all(split_view, 'io', split_axis=1, concat_axis=0, tiled=True)  11 us
    reshape x1, local copies, waits for them, and re-layouts, local(): split_view = snapshots.reshape(local_rows, groups, lon_dev)  10.7 us
    dot_general x1, matrix products, fit_block(): moments = jnp.dot(basis.T, series, precision=lax.Precision.HIGHEST)  6.06 us
    dot_general x1, matrix products, fit_block(): coeffs = jnp.dot(projector, series, precision=lax.Precision.HIGHEST)  5.99 us
    reduce_sum x1, other arithmetic, fit_block(): total = jnp.sum(series * series, axis=0)  5.79 us
  transfers between devices with their start and end apart: 1, of which 1 were waited for; matrix products, arithmetic and copies ran while one was open for 2% of the time, Pallas kernels for 0%

commit v1 on v0

v1 whole, which is shorter than its diff:
```python
import functools

import jax
import jax.numpy as jnp
import numpy as np
from jax import lax
from jax.experimental import pallas as pl
from jax.experimental.pallas import tpu as pltpu
from jax.sharding import PartitionSpec as P

TIMES = 96
HARM = 16
MONTHS = 12
EXTRA = 4
UNITS = 8
STAGES = 6
FLOWS = (("P", 1, 3), ("P", 3, 1), ("Q", 1, 3), ("Q", 3, 1))


def constants():
    steps = np.arange(TIMES, dtype=np.float64)
    columns = [np.ones_like(steps), (steps - (TIMES - 1) / 2.0) / (TIMES / 2.0)]
    for harmonic in range(1, 7):
        columns.append(np.cos(2.0 * np.pi * harmonic * steps / 12.0))
    for harmonic in range(1, 6):
        columns.append(np.sin(2.0 * np.pi * harmonic * steps / 12.0))
    columns.append(np.cos(2.0 * np.pi * steps / TIMES))
    columns.append(np.sin(2.0 * np.pi * steps / TIMES))
    columns.append(np.cos(4.0 * np.pi * steps / TIMES))
    basis = np.stack(columns, axis=1)
    others = (1, 13, 14, 15)
    gather = np.zeros((HARM, MONTHS + EXTRA))
    for row in range(HARM):
        if row in others:
            gather[row, MONTHS + others.index(row)] = 1.0
        else:
            gather[row, :MONTHS] = basis[:MONTHS, row]
    gram = basis.T @ basis
    fit = np.linalg.solve(gram, gather)
    root = np.linalg.cholesky(gather.T @ fit)
    table = basis[:, others]
    return table, fit, root


def flip(v, mask):
    if mask == 1:
        return v + 1 - 2 * lax.rem(v, 2)
    if mask == 3:
        return 3 - v
    return lax.rem(v + 2, 4)


def flow_shapes(kind):
    tile = (8, 128)
    if kind == "P":
        dims = {
            "own": (2, 3, 4, 2),
            "r1": (2, 3, 4, 2),
            "r2": (2, 3, 4, 2),
            "s8": (4, 2, 8),
            "r3": (2, 2, 8),
            "sum": (2, 2, 11),
            "r4": (2, 11),
            "r5": (11,),
            "out": (17,),
        }
    else:
        dims = {
            "own": (2, 3, 4, 2),
            "r1": (2, 3, 4, 2),
            "r2": (2, 3, 4, 2),
            "r3": (4, 3, 4),
            "sum": (4, 17),
            "r4": (2, 17),
            "r5": (17,),
            "out": (17,),
        }
    return {name: (UNITS,) + dim + tile for name, dim in dims.items()}


SEMS = ("ownl", "ownr", "r1", "r2", "r3", "r4", "r5")


def scratch():
    shapes = []
    for kind, _, _ in FLOWS:
        for shape in flow_shapes(kind).values():
            shapes.append(pltpu.VMEM(shape, jnp.float32))
        for _ in SEMS:
            shapes.append(pltpu.SemaphoreType.DMA((UNITS,)))
        shapes.append(pltpu.SemaphoreType.DMA((STAGES,)))
    shapes.append(pltpu.SemaphoreType.DMA((3, 2)))
    return shapes


def kernel(fit, root, table_ref, x_ref, coef_ref, var_ref, *refs):
    me = lax.axis_index("io")
    core = lax.rem(me, 2)
    y = lax.rem(lax.div(me, 2), 2)
    x = lax.rem(lax.div(me, 4), 4)
    z = lax.div(me, 16)
    parity = lax.rem(x, 2)

    def dev(zz, xx, yy, cc):
        return ((zz * 4 + xx) * 2 + yy) * 2 + cc

    refs = list(refs)
    out_sem = refs.pop()
    flows = []
    at = 0
    for number, (kind, first, second) in enumerate(FLOWS):
        flow = {"kind": kind, "f": first, "g": second, "number": number}
        for name in flow_shapes(kind):
            flow[name] = refs[at]
            at += 1
        flow["sem"] = {}
        for name in SEMS:
            flow["sem"][name] = refs[at]
            at += 1
        flow["send"] = refs[at]
        at += 1
        flows.append(flow)

    def push(src, dst, send, recv, device):
        pltpu.make_async_remote_copy(
            src_ref=src,
            dst_ref=dst,
            send_sem=send,
            recv_sem=recv,
            device_id={"io": device},
            device_id_type=pl.DeviceIdType.MESH,
        ).start()

    def await_bytes(ref, sem):
        pltpu.make_async_copy(ref, ref, sem).wait()

    barrier = pltpu.get_barrier_semaphore()
    friends = [dev(z, x, y, 1 - core), dev(z, x, 1 - y, core)]
    for mask in (1, 3):
        for c in (core, 1 - core):
            friends.append(dev(flip(z, mask), x, y, c))
            friends.append(dev(z, flip(x, mask), y, c))
    for friend in friends:
        pl.semaphore_signal(barrier, inc=1, device_id={"io": friend}, device_id_type=pl.DeviceIdType.MESH)
    pl.semaphore_wait(barrier, len(friends))

    def place(flow, i):
        return flow["number"] * (UNITS // 2) + lax.div(i, 2), lax.rem(i, 2)

    def begin(flow, i):
        lat, half = place(flow, i)
        sem = flow["sem"]
        along_z = flow["kind"] == "P"
        here = z if along_z else x
        there = flip(here, flow["f"])
        for at_home in (False, True):
            spot = here if at_home else there
            zz, xx = (spot, x) if along_z else (z, spot)
            for slot, block in ((0, spot), (1, flip(spot, flow["g"]))):
                for group, when in ((0, core), (2, core + 1), (1, 2 * core)):
                    if along_z:
                        src = x_ref.at[group, lat, block, :, :, half]
                    else:
                        src = x_ref.at[group, lat, :, block, :, half]
                    c = 1 - core if group == 1 else core
                    if not at_home:
                        push(src, flow["r1"].at[i, slot, when], flow["send"].at[0], sem["r1"].at[i], dev(zz, xx, y, c))
                    elif group == 1:
                        push(src, flow["own"].at[i, slot, when], flow["send"].at[5], sem["ownr"].at[i], dev(zz, xx, y, c))
                    else:
                        pltpu.make_async_copy(src, flow["own"].at[i, slot, when], sem["ownl"].at[i]).start()

    def second(flow, i):
        sem = flow["sem"]
        await_bytes(flow["own"].at[i, :, 0:2], sem["ownl"].at[i])
        await_bytes(flow["own"].at[i, :, 0], sem["ownr"].at[i])
        await_bytes(flow["r1"].at[i], sem["r1"].at[i])
        if flow["kind"] == "P":
            to = dev(flip(z, flow["g"]), x, y, core)
        else:
            to = dev(z, flip(x, flow["g"]), y, core)
        push(flow["own"].at[i, 1], flow["r2"].at[i, 0], flow["send"].at[1], sem["r2"].at[i], to)
        push(flow["r1"].at[i, 1], flow["r2"].at[i, 1], flow["send"].at[1], sem["r2"].at[i], to)

    def weights(chip, k):
        base = (chip * 3 + k) * EXTRA
        return [table_ref[base + j] for j in range(EXTRA)]

    def gather_stats(pieces):
        sums, moments, total = {}, [None] * EXTRA, None
        for key, k, value, w in pieces:
            sums[key, k] = value if (key, k) not in sums else sums[key, k] + value
            for j in range(EXTRA):
                term = w[j] * value
                moments[j] = term if moments[j] is None else moments[j] + term
            square = value * value
            total = square if total is None else total + square
        return sums, moments, total

    def third_p(flow, i):
        sem = flow["sem"]
        await_bytes(flow["r2"].at[i], sem["r2"].at[i])
        own, r1, r2, s8 = flow["own"], flow["r1"], flow["r2"], flow["s8"]
        f, g = flow["f"], flow["g"]
        lines = (z, flip(z, f), flip(z, g), flip(z, 2))
        for xs, xb in enumerate((x, flip(x, g), flip(x, f), flip(x, 2))):
            for ys, yb in enumerate((y, 1 - y)):
                pieces = []
                for k in range(3):
                    values = (own[i, 0, k, xb, yb], r1[i, 0, k, xb, yb], r2[i, 0, k, xb, yb], r2[i, 1, k, xb, yb])
                    for line, value in zip(lines, values):
                        pieces.append((0, k, value, weights(line * 8 + x * 2 + y, k)))
                sums, moments, total = gather_stats(pieces)
                for k in range(3):
                    s8[i, xs, ys, k] = sums[0, k]
                for j in range(EXTRA):
                    s8[i, xs, ys, 3 + j] = moments[j]
                s8[i, xs, ys, 7] = total
        push(s8.at[i, 2:4], flow["r3"].at[i], flow["send"].at[2], sem["r3"].at[i], dev(z, flip(x, f), y, core))

    def fourth_p(flow, i):
        sem = flow["sem"]
        await_bytes(flow["r3"].at[i], sem["r3"].at[i])
        s8, r3, acc = flow["s8"], flow["r3"], flow["sum"]
        for s in (1, 0):
            for ys in range(2):
                for k in range(3):
                    acc[i, s, ys, 3 * parity + k] = s8[i, s, ys, k]
                    acc[i, s, ys, 3 * (1 - parity) + k] = r3[i, s, ys, k]
                for j in range(EXTRA + 1):
                    acc[i, s, ys, 6 + j] = s8[i, s, ys, 3 + j] + r3[i, s, ys, 3 + j]
        push(acc.at[i, 1], flow["r4"].at[i], flow["send"].at[3], sem["r4"].at[i], dev(z, flip(x, flow["g"]), y, core))

    def fifth_p(flow, i):
        sem = flow["sem"]
        await_bytes(flow["r4"].at[i], sem["r4"].at[i])
        acc, r4 = flow["sum"], flow["r4"]
        for ys in (1, 0):
            acc[i, 0, ys] = acc[i, 0, ys] + r4[i, ys]
        push(acc.at[i, 0, 1], flow["r5"].at[i], flow["send"].at[4], sem["r5"].at[i], dev(z, x, 1 - y, core))

    def third_q(flow, i):
        sem = flow["sem"]
        await_bytes(flow["r2"].at[i], sem["r2"].at[i])
        to = dev(z, x, 1 - y, core)
        other = 1 - y
        r3 = flow["r3"]
        push(flow["own"].at[i, 0, :, :, other], r3.at[i, 0], flow["send"].at[2], sem["r3"].at[i], to)
        push(flow["r1"].at[i, 0, :, :, other], r3.at[i, 1], flow["send"].at[2], sem["r3"].at[i], to)
        push(flow["r2"].at[i, 0, :, :, other], r3.at[i, 2], flow["send"].at[2], sem["r3"].at[i], to)
        push(flow["r2"].at[i, 1, :, :, other], r3.at[i, 3], flow["send"].at[2], sem["r3"].at[i], to)

    def fourth_q(flow, i):
        sem = flow["sem"]
        await_bytes(flow["r3"].at[i], sem["r3"].at[i])
        own, r1, r2, r3, acc = flow["own"], flow["r1"], flow["r2"], flow["r3"], flow["sum"]
        f, g = flow["f"], flow["g"]
        spots = (x, flip(x, f), flip(x, g), flip(x, 2))
        same = (0, 1, 1, 0)
        for zs, zb in enumerate((z, flip(z, g), flip(z, f), flip(z, 2))):
            pieces = []
            for k in range(3):
                near = (own[i, 0, k, zb, y], r1[i, 0, k, zb, y], r2[i, 0, k, zb, y], r2[i, 1, k, zb, y])
                far = tuple(r3[i, s, k, zb] for s in range(4))
                for b, (values, yy) in enumerate(((near, y), (far, 1 - y))):
                    for s in range(4):
                        pieces.append(((same[s], b), k, values[s], weights(z * 8 + spots[s] * 2 + yy, k)))
            sums, moments, total = gather_stats(pieces)
            for a, xl in enumerate((parity, 1 - parity)):
                for b, yy in enumerate((y, 1 - y)):
                    for k in range(3):
                        acc[i, zs, 3 * (2 * xl + yy) + k] = sums[(a, b), k]
            for j in range(EXTRA):
                acc[i, zs, MONTHS + j] = moments[j]
            acc[i, zs, MONTHS + EXTRA] = total
        push(acc.at[i, 2:4], flow["r4"].at[i], flow["send"].at[3], sem["r4"].at[i], dev(flip(z, f), x, y, core))

    def fifth_q(flow, i):
        sem = flow["sem"]
        await_bytes(flow["r4"].at[i], sem["r4"].at[i])
        acc, r4 = flow["sum"], flow["r4"]
        for s in (1, 0):
            acc[i, s] = acc[i, s] + r4[i, s]
        push(acc.at[i, 1], flow["r5"].at[i], flow["send"].at[4], sem["r5"].at[i], dev(flip(z, flow["g"]), x, y, core))

    def finish(flow, i):
        sem = flow["sem"]
        await_bytes(flow["r5"].at[i], sem["r5"].at[i])
        acc, r5, out = flow["sum"], flow["r5"], flow["out"]
        if flow["kind"] == "P":
            w = [None] * (MONTHS + EXTRA)
            low = y == 0
            for xl in range(2):
                for k in range(3):
                    mine, theirs = acc[i, 0, 0, 3 * xl + k], r5[i, 3 * xl + k]
                    w[6 * xl + k] = jnp.where(low, mine, theirs)
                    w[6 * xl + 3 + k] = jnp.where(low, theirs, mine)
            for j in range(EXTRA):
                w[MONTHS + j] = acc[i, 0, 0, 6 + j] + r5[i, 6 + j]
            total = acc[i, 0, 0, 10] + r5[i, 10]
        else:
            w = [acc[i, 0, j] + r5[i, j] for j in range(MONTHS + EXTRA)]
            total = acc[i, 0, MONTHS + EXTRA] + r5[i, MONTHS + EXTRA]
        for row in range(HARM):
            value = None
            for j in range(MONTHS + EXTRA):
                term = w[j] * float(np.float32(fit[row, j]))
                value = term if value is None else value + term
            out[i, row] = value
        explained = None
        for col in range(HARM):
            value = None
            for j in range(col, HARM):
                if abs(root[j, col]) < 1e-12:
                    continue
                term = w[j] * float(np.float32(root[j, col]))
                value = term if value is None else value + term
            explained = value * value if explained is None else explained + value * value
        out[i, HARM] = (total - explained) * (1.0 / TIMES)
        lat, half = place(flow, i)
        row = core * 16 + lat

        @pl.when(half == core)
        def _():
            pltpu.make_async_copy(out.at[i, 0:HARM], coef_ref.at[:, row], out_sem.at[0, 0]).start()
            pltpu.make_async_copy(out.at[i, HARM], var_ref.at[row], out_sem.at[0, 1]).start()

        @pl.when(half != core)
        def _():
            to = dev(z, x, y, 1 - core)
            push(out.at[i, 0:HARM], coef_ref.at[:, row], out_sem.at[1, 0], out_sem.at[2, 0], to)
            push(out.at[i, HARM], var_ref.at[row], out_sem.at[1, 1], out_sem.at[2, 1], to)

    steps = {
        "P": (begin, second, third_p, fourth_p, fifth_p, finish),
        "Q": (begin, second, third_q, fourth_q, fifth_q, finish),
    }

    @pl.loop(0, UNITS + STAGES - 1)
    def _(turn):
        for stage in range(STAGES):
            for flow in flows:
                unit = turn - stage

                @pl.when((unit >= 0) & (unit < UNITS))
                def _(flow=flow, stage=stage, unit=unit):
                    steps[flow["kind"]][stage](flow, unit)

    for flow in flows:
        for stage in range(5):
            await_bytes(flow[f"r{stage + 1}"], flow["send"].at[stage])
        await_bytes(flow["own"].at[:, :, 0], flow["send"].at[5])
    for k in range(3):
        await_bytes(coef_ref.at[:, 0:16], out_sem.at[k, 0])
        await_bytes(var_ref.at[0:16], out_sem.at[k, 1])


def local(snapshots):
    table, fit, root = constants()
    tiles = snapshots.reshape(48, 8, 64, 128).transpose(0, 2, 1, 3)
    tiles = tiles.reshape(3, 16, 4, 4, 2, 2, 8, 128)
    coeffs, variance = pl.pallas_call(
        functools.partial(kernel, fit, root),
        out_shape=(
            jax.ShapeDtypeStruct((HARM, 32, 8, 128), jnp.float32),
            jax.ShapeDtypeStruct((32, 8, 128), jnp.float32),
        ),
        in_specs=[pl.BlockSpec(memory_space=pltpu.SMEM), pl.BlockSpec(memory_space=pl.ANY)],
        out_specs=(pl.BlockSpec(memory_space=pl.ANY), pl.BlockSpec(memory_space=pl.ANY)),
        scratch_shapes=scratch(),
        compiler_params=pltpu.CompilerParams(
            collective_id=0, has_side_effects=True, vmem_limit_bytes=60 * 1024 * 1024
        ),
    )(jnp.asarray(table.reshape(-1), dtype=jnp.float32), tiles)
    return coeffs.reshape(HARM, 256, 128), variance.reshape(256, 128)


def solution(mesh):
    return jax.shard_map(
        local,
        mesh=mesh,
        in_specs=(P(("rep", "io"), None),),
        out_specs=(P("rep", None, "io"), P("rep", "io")),
        check_vma=False,
    )
```

time: 229 us -> 133 us (0.58)
  waiting for transfers between devices: 164 us -> 0 us
  Pallas kernels: 0 us -> 128 us
  local copies, waits for them, and re-layouts: 28.8 us -> 3.81 us
  matrix products: 12.5 us -> 0 us
  starting transfers between devices: 11 us -> 0 us
  other arithmetic: 10.9 us -> 0 us
    all_to_all x1 -> x0, waiting for transfers between devices: 164 us -> none  [local(): lax.all_to_all(split_view, 'io', split_axis=1, concat_axis=0, tiled=True)]
    pallas_call x0 -> x1, Pallas kernels: none -> 128 us  [local(): pl.pallas_call(functools.partial(kernel, fit, root), out_shape=(jax.Shape...]
    another operation x3 -> x0, local copies, waits for them, and re-layouts: 13.9 us -> none  [the longest x1 13.8 us: fit_block(): series = block.reshape(TIMES, lat_rows * width)]
    dot_general x3 -> x0, matrix products: 12.2 us -> none  [the longest x1 6.06 us: fit_block(): moments = jnp.dot(basis.T, series, precision=lax.Precision.HIGHEST)]
    all_to_all x1 -> x0, starting transfers between devices: 11 us -> none  [local(): lax.all_to_all(split_view, 'io', split_axis=1, concat_axis=0, tiled=True)]
    reshape x1 -> x0, local copies, waits for them, and re-layouts: 10.7 us -> none  [local(): split_view = snapshots.reshape(local_rows, groups, lon_dev)]
    reduce_sum x1 -> x0, other arithmetic: 5.79 us -> none  [fit_block(): total = jnp.sum(series * series, axis=0)]
    another operation x5 -> x0, other arithmetic: 4.02 us -> none  [the longest x3 2.14 us: projector_of(): factor = jnp.linalg.cholesky(gram)]
  transfers between devices with their start and end apart: 1 -> 0, of which waited for: 1 -> 0; matrix products, arithmetic and copies ran while one was open for 2% -> 0% of each run, Pallas kernels for 0% -> 0%
where the time goes in v1:
time: 133 us; the launch traced here: 132 us
  Pallas kernels  128 us (96%)
  local copies, waits for them, and re-layouts  3.81 us (3%)
    pallas_call x1, Pallas kernels, local(): pl.pallas_call(functools.partial(kernel, fit, root), out_shape=(jax.Shape...  128 us
    unnamed x4, local copies, waits for them, and re-layouts  3.81 us

profile of v1, /device:TPU:1, one launch (start us, length us, event | category | flops | bytes accessed | tf_op | source)
XLA Modules:
  0.0 132.3 jit_solution(13858860233484962457)
XLA Ops:
  0.6 127.9 %shard_map.41 = (f32[16,32,8,128]{3,2,1,0:T(8,128)}, f32[32,8,128]{2,1,0:T(8,128)}) custom-call(f32[384]{0:T(512)} %constant.2.clone.table_ref, f32[3,16,4,4,2,2,8,128]{7,6,5,4,3,2,1,0:T(8,128)} %bitcast.7), custom_call_target="tpu_custom_call" | custom-call | tf_op jit(solution)/shard_map/pallas_call | solution.py:362
  128.5 0.0 copy-start
  128.5 3.1 %copy.6 = f32[16,256,128]{2,1,0:T(8,128)} copy(f32[16,256,128]{2,1,0:T(8,128)} %bitcast.8) | data formatting | bytes 4194304
  131.7 0.0 copy-done
  131.7 0.7 copy.7
Async XLA Ops:
  128.5 3.2 %copy-start = (f32[32,8,128]{2,1,0:T(8,128)S(1)}, f32[32,8,128]{2,1,0:T(8,128)}, u32[]{:S(2)}) copy-start(f32[32,8,128]{2,1,0:T(8,128)} %get-tuple-element.5) | copy-start | bytes 393220

commit v2 on v1

v2 whole, which is shorter than its diff:
```python
import functools

import jax
import jax.numpy as jnp
import numpy as np
from jax import lax
from jax.experimental import pallas as pl
from jax.experimental.pallas import tpu as pltpu
from jax.sharding import PartitionSpec as P

TIMES = 96
HARM = 16
MONTHS = 12
EXTRA = 4
STAGES = 6
VMEM_LIMIT = 60817408
FLOWS = (
    ("zz", 1, "xyx", 1),
    ("zz", 3, "xxy", 3),
    ("xx", 1, "yzz", 1),
    ("xx", 3, "yzz", 3),
)
UNITS = (8, 8, 8, 8)
DELAY = (
    (6, 11, 14, 21, 26, 29),
    (7, 8, 17, 20, 29, 59),
    (5, 9, 12, 16, 26, 29),
    (6, 9, 12, 16, 20, 32),
)
KEY = (
    (20, 21, 22, 6, 0, 11),
    (3, 17, 14, 19, 13, 5),
    (23, 4, 8, 9, 2, 1),
    (7, 15, 12, 10, 18, 16),
)


def constants():
    steps = np.arange(TIMES, dtype=np.float64)
    columns = [np.ones_like(steps), (steps - (TIMES - 1) / 2.0) / (TIMES / 2.0)]
    for harmonic in range(1, 7):
        columns.append(np.cos(2.0 * np.pi * harmonic * steps / 12.0))
    for harmonic in range(1, 6):
        columns.append(np.sin(2.0 * np.pi * harmonic * steps / 12.0))
    columns.append(np.cos(2.0 * np.pi * steps / TIMES))
    columns.append(np.sin(2.0 * np.pi * steps / TIMES))
    columns.append(np.cos(4.0 * np.pi * steps / TIMES))
    basis = np.stack(columns, axis=1)
    others = (1, 13, 14, 15)
    gather = np.zeros((HARM, MONTHS + EXTRA))
    for row in range(HARM):
        if row in others:
            gather[row, MONTHS + others.index(row)] = 1.0
        else:
            gather[row, :MONTHS] = basis[:MONTHS, row]
    gram = basis.T @ basis
    fit = np.linalg.solve(gram, gather)
    root = np.linalg.cholesky(gather.T @ fit)
    table = basis[:, others]
    return table, fit, root


def flip(v, mask):
    if mask == 1:
        return v + 1 - 2 * lax.rem(v, 2)
    if mask == 3:
        return 3 - v
    return lax.rem(v + 2, 4)

def plan(flow):
    raw, _, post, _ = flow
    merged = {"x"} if raw == "xx" else set()
    values = 11 if raw == "xx" else 8
    rows = []
    for axis in post:
        joins = axis in ("x", "y") and axis not in merged
        after = values
        if joins:
            after = values + (3 if not merged else 6)
        rows.append((axis, values, after, tuple(sorted(merged)), joins))
        if joins:
            merged.add(axis)
        values = after
    return rows


def flow_shapes(number):
    units = UNITS[number]
    rows = plan(FLOWS[number])
    dims = {"own": (2, 3, 4, 2), "r1": (2, 3, 4, 2), "r2": (2, 3, 4, 2)}
    dims["s0"] = (2, 2, 2, rows[0][1])
    blocks = (2, 2, 2)
    for at, (_, before, after, _, joins) in enumerate(rows):
        blocks = blocks[1:]
        dims[f"r{at + 3}"] = blocks + (before,)
        if joins:
            dims[f"s{at + 1}"] = blocks + (after,)
    dims["out"] = (HARM + 1,)
    return {name: (units,) + dim + (8, 128) for name, dim in dims.items()}


SEMS = ("ownl", "ownr", "r1", "r2", "r3", "r4", "r5")


def scratch():
    shapes = []
    for number in range(len(FLOWS)):
        for shape in flow_shapes(number).values():
            shapes.append(pltpu.VMEM(shape, jnp.float32))
        for _ in SEMS:
            shapes.append(pltpu.SemaphoreType.DMA((UNITS[number],)))
        shapes.append(pltpu.SemaphoreType.DMA((STAGES,)))
    shapes.append(pltpu.SemaphoreType.DMA((2, 2)))
    return shapes


def kernel(fit, root, table_ref, x_ref, coef_ref, var_ref, *refs):
    me = lax.axis_index("io")
    core = lax.rem(me, 2)
    y = lax.rem(lax.div(me, 2), 2)
    x = lax.rem(lax.div(me, 4), 4)
    z = lax.div(me, 16)
    parity = lax.rem(x, 2)

    def dev(zz, xx, yy, cc):
        return ((zz * 4 + xx) * 2 + yy) * 2 + cc

    refs = list(refs)
    out_sem = refs.pop()
    flows = []
    at, base = 0, 0
    for number, spec in enumerate(FLOWS):
        raw, first, post, ring = spec
        flow = {"raw": raw, "f": first, "g": 4 - first, "post": post, "pf": ring, "pg": 4 - ring}
        flow["base"], flow["units"], flow["rows"] = base, UNITS[number], plan(spec)
        base += UNITS[number]
        for name in flow_shapes(number):
            flow[name] = refs[at]
            at += 1
        flow["sem"] = {}
        for name in SEMS:
            flow["sem"][name] = refs[at]
            at += 1
        flow["send"] = refs[at]
        at += 1
        flows.append(flow)

    def push(src, dst, send, recv, device):
        pltpu.make_async_remote_copy(
            src_ref=src,
            dst_ref=dst,
            send_sem=send,
            recv_sem=recv,
            device_id={"io": device},
            device_id_type=pl.DeviceIdType.MESH,
        ).start()

    def await_bytes(ref, sem):
        pltpu.make_async_copy(ref, ref, sem).wait()

    barrier = pltpu.get_barrier_semaphore()
    friends = [dev(z, x, y, 1 - core), dev(z, x, 1 - y, core)]
    for mask in (1, 3):
        for c in (core, 1 - core):
            friends.append(dev(flip(z, mask), x, y, c))
            friends.append(dev(z, flip(x, mask), y, c))
    for friend in friends:
        pl.semaphore_signal(barrier, inc=1, device_id={"io": friend}, device_id_type=pl.DeviceIdType.MESH)
    pl.semaphore_wait(barrier, len(friends))

    def place(flow, i):
        unit = flow["base"] + i
        return lax.div(unit, 2), lax.rem(unit, 2)

    def begin(flow, i):
        lat, half = place(flow, i)
        sem = flow["sem"]
        along_z = flow["raw"] == "zz"
        here = z if along_z else x
        there = flip(here, flow["f"])
        for at_home in (False, True):
            spot = here if at_home else there
            zz, xx = (spot, x) if along_z else (z, spot)
            for slot, block in ((0, spot), (1, flip(spot, flow["g"]))):
                for group, when in ((0, core), (2, core + 1), (1, 2 * core)):
                    if along_z:
                        src = x_ref.at[group, lat, block, :, :, half]
                    else:
                        src = x_ref.at[group, lat, :, block, :, half]
                    c = 1 - core if group == 1 else core
                    if not at_home:
                        push(src, flow["r1"].at[i, slot, when], flow["send"].at[0], sem["r1"].at[i], dev(zz, xx, y, c))
                    elif group == 1:
                        push(src, flow["own"].at[i, slot, when], flow["send"].at[5], sem["ownr"].at[i], dev(zz, xx, y, c))
                    else:
                        pltpu.make_async_copy(src, flow["own"].at[i, slot, when], sem["ownl"].at[i]).start()

    def second(flow, i):
        sem = flow["sem"]
        await_bytes(flow["own"].at[i, :, 0:2], sem["ownl"].at[i])
        await_bytes(flow["own"].at[i, :, 0], sem["ownr"].at[i])
        await_bytes(flow["r1"].at[i], sem["r1"].at[i])
        if flow["raw"] == "zz":
            to = dev(flip(z, flow["g"]), x, y, core)
        else:
            to = dev(z, flip(x, flow["g"]), y, core)
        push(flow["own"].at[i, 1], flow["r2"].at[i, 0], flow["send"].at[1], sem["r2"].at[i], to)
        push(flow["r1"].at[i, 1], flow["r2"].at[i, 1], flow["send"].at[1], sem["r2"].at[i], to)

    def partner(flow, stage):
        axis = flow["post"][stage]
        if axis == "y":
            return dev(z, x, 1 - y, core)
        mask = flow["pg"] if axis in flow["post"][:stage] else flow["pf"]
        if axis == "x":
            return dev(z, flip(x, mask), y, core)
        return dev(flip(z, mask), x, y, core)

    def send_stats(flow, i, stage, state):
        name = f"r{stage + 3}"
        push(state.at[1], flow[name].at[i], flow["send"].at[stage + 2], flow["sem"][name].at[i], partner(flow, stage))

    def weights(chip, k):
        base = (chip * 3 + k) * EXTRA
        return [table_ref[base + j] for j in range(EXTRA)]

    def reduce_raw(flow, i):
        await_bytes(flow["r2"].at[i], flow["sem"]["r2"].at[i])
        own, r1, r2, s0 = flow["own"], flow["r1"], flow["r2"], flow["s0"]
        f, g, post = flow["f"], flow["g"], flow["post"]
        along_z = flow["raw"] == "zz"
        here = z if along_z else x
        spots = (here, flip(here, f), flip(here, g), flip(here, 2))
        chips = [spot * 8 + x * 2 + y if along_z else z * 8 + spot * 2 + y for spot in spots]
        across = x if along_z else z
        ring = "x" if along_z else "z"
        for b0 in (1, 0):
            for b1 in range(2):
                for b2 in range(2):
                    bits = (b0, b1, b2)
                    lon, lon_y, seen = 0, y, False
                    for bit, axis in zip(bits, post):
                        if axis == "y":
                            lon_y = 1 - y if bit else y
                        else:
                            lon = lon ^ (bit * (flow["pg"] if seen else flow["pf"]))
                            seen = True
                    block = across if lon == 0 else flip(across, lon)
                    sums, moments, total = {}, [None] * EXTRA, None
                    for k in range(3):
                        values = (
                            own[i, 0, k, block, lon_y],
                            r1[i, 0, k, block, lon_y],
                            r2[i, 0, k, block, lon_y],
                            r2[i, 1, k, block, lon_y],
                        )
                        for number, value in enumerate(values):
                            key = (0 if along_z or number in (0, 3) else 1, k)
                            sums[key] = value if key not in sums else sums[key] + value
                            w = weights(chips[number], k)
                            for j in range(EXTRA):
                                term = w[j] * value
                                moments[j] = term if moments[j] is None else moments[j] + term
                            square = value * value
                            total = square if total is None else total + square
                    for (a, k), value in sums.items():
                        if along_z:
                            s0[i, b0, b1, b2, k] = value
                        else:
                            s0[i, b0, b1, b2, 3 * (1 - parity if a else parity) + k] = value
                    months = 3 if along_z else 6
                    for j in range(EXTRA):
                        s0[i, b0, b1, b2, months + j] = moments[j]
                    s0[i, b0, b1, b2, months + EXTRA] = total
        send_stats(flow, i, 0, s0.at[i])

    def merge(flow, i, stage):
        name = f"r{stage + 3}"
        await_bytes(flow[name].at[i], flow["sem"][name].at[i])
        axis, before, after, merged, joins = flow["rows"][stage]
        theirs = flow[name].at[i]
        mine = flow["state"].at[0]
        blocks = [()]
        for _ in range(2 - stage):
            blocks = [b + (bit,) for b in blocks for bit in (1, 0)]
        if not joins:
            for b in blocks:
                mine[b] = mine[b] + theirs[b]
            return mine
        new = flow[f"s{stage + 1}"].at[i]
        own_class = parity if axis == "x" else y
        months = before - EXTRA - 1
        for b in blocks:
            for k in range(months):
                if not merged:
                    spot = [3 * c + k for c in (own_class, 1 - own_class)]
                elif axis == "y":
                    spot = [6 * (k // 3) + 3 * c + k % 3 for c in (own_class, 1 - own_class)]
                else:
                    spot = [6 * c + k for c in (own_class, 1 - own_class)]
                new[b + (spot[0],)] = mine[b + (k,)]
                new[b + (spot[1],)] = theirs[b + (k,)]
            for j in range(EXTRA + 1):
                new[b + (2 * months + j,)] = mine[b + (months + j,)] + theirs[b + (months + j,)]
        return new

    def exchange(flow, i, stage):
        flow["state"] = flow["s0"].at[i]
        for done in range(stage - 1):
            joins = flow["rows"][done][4]
            flow["state"] = flow[f"s{done + 1}"].at[i] if joins else flow["state"].at[0]
        state = merge(flow, i, stage - 1)
        if stage < 3:
            send_stats(flow, i, stage, state)
        return state

    def finish(flow, i):
        state = exchange(flow, i, 3)
        out = flow["out"]
        w = [state[j] for j in range(MONTHS + EXTRA)]
        total = state[MONTHS + EXTRA]
        for row in range(HARM):
            value = None
            for j in range(MONTHS + EXTRA):
                term = w[j] * float(np.float32(fit[row, j]))
                value = term if value is None else value + term
            out[i, row] = value
        explained = None
        for col in range(HARM):
            value = None
            for j in range(col, HARM):
                if abs(root[j, col]) < 1e-12:
                    continue
                term = w[j] * float(np.float32(root[j, col]))
                value = term if value is None else value + term
            explained = value * value if explained is None else explained + value * value
        out[i, HARM] = (total - explained) * (1.0 / TIMES)
        lat, half = place(flow, i)
        row = core * 16 + lat

        @pl.when(half != core)
        def _():
            to = dev(z, x, y, 1 - core)
            push(out.at[i, 0:HARM], coef_ref.at[:, row], out_sem.at[0, 0], out_sem.at[1, 0], to)
            push(out.at[i, HARM], var_ref.at[row], out_sem.at[0, 1], out_sem.at[1, 1], to)

        @pl.when(half == core)
        def _():
            for k in range(HARM):
                coef_ref[k, row] = out[i, k]
            var_ref[row] = out[i, HARM]

    def step(flow, stage, i):
        if stage == 0:
            begin(flow, i)
        elif stage == 1:
            second(flow, i)
        elif stage == 2:
            reduce_raw(flow, i)
        elif stage == 5:
            finish(flow, i)
        else:
            exchange(flow, i, stage - 2)

    order = sorted((KEY[f][s], f, s) for f in range(len(FLOWS)) for s in range(STAGES))

    @pl.loop(0, max(u + max(d) for u, d in zip(UNITS, DELAY)))
    def _(turn):
        for _, number, stage in order:
            flow = flows[number]
            unit = turn - DELAY[number][stage]

            @pl.when((unit >= 0) & (unit < flow["units"]))
            def _(flow=flow, stage=stage, unit=unit):
                step(flow, stage, unit)

    for flow in flows:
        for stage in range(5):
            await_bytes(flow[f"r{stage + 1}"], flow["send"].at[stage])
        await_bytes(flow["own"].at[:, :, 0], flow["send"].at[5])
    for k in range(2):
        await_bytes(coef_ref.at[:, 0:16], out_sem.at[k, 0])
        await_bytes(var_ref.at[0:16], out_sem.at[k, 1])


def local(snapshots):
    table, fit, root = constants()
    tiles = snapshots.reshape(48, 8, 64, 128).transpose(0, 2, 1, 3)
    tiles = tiles.reshape(3, 16, 4, 4, 2, 2, 8, 128)
    coeffs, variance = pl.pallas_call(
        functools.partial(kernel, fit, root),
        out_shape=(
            pltpu.VMEM((HARM, 32, 8, 128), jnp.float32),
            pltpu.VMEM((32, 8, 128), jnp.float32),
        ),
        in_specs=[pl.BlockSpec(memory_space=pltpu.SMEM), pl.BlockSpec(memory_space=pl.ANY)],
        out_specs=(pl.BlockSpec(memory_space=pltpu.VMEM), pl.BlockSpec(memory_space=pltpu.VMEM)),
        scratch_shapes=scratch(),
        compiler_params=pltpu.CompilerParams(
            collective_id=0, has_side_effects=True, vmem_limit_bytes=VMEM_LIMIT
        ),
    )(jnp.asarray(table.reshape(-1), dtype=jnp.float32), tiles)
    return coeffs.reshape(HARM, 256, 128), variance.reshape(256, 128)


def solution(mesh):
    return jax.shard_map(
        local,
        mesh=mesh,
        in_specs=(P(("rep", "io"), None),),
        out_specs=(P("rep", None, "io"), P("rep", "io")),
        check_vma=False,
    )
```

time: 133 us -> 130 us (0.977)
  local copies, waits for them, and re-layouts: 3.81 us -> 1.98 us
    unnamed x4 -> x2, local copies, waits for them, and re-layouts: 3.81 us -> 1.98 us
where the time goes in v2:
time: 130 us
  Pallas kernels  127 us (98%)
  local copies, waits for them, and re-layouts  1.98 us (2%)
    pallas_call x1, Pallas kernels, local(): pl.pallas_call(functools.partial(kernel, fit, root), out_shape=(pltpu.VME...  127 us

profile of v2, /device:TPU:1, one launch (start us, length us, event | category | flops | bytes accessed | tf_op | source)
XLA Modules:
  0.0 129.5 jit_solution(15715683886415817011)
XLA Ops:
  0.6 126.9 %shard_map.41 = (f32[16,32,8,128]{3,2,1,0:T(8,128)S(1)}, f32[32,8,128]{2,1,0:T(8,128)S(1)}) custom-call(f32[384]{0:T(512)} %constant.2.clone.table_ref, f32[3,16,4,4,2,2,8,128]{7,6,5,4,3,2,1,0:T(8,128)} %bitcast.9), custom_call_target="tpu_custom_call" | custom-call | tf_op jit(solution)/shard_map/pallas_call | solution.py:390
  127.5 1.3 %copy.6 = f32[16,256,128]{2,1,0:T(8,128)} copy(f32[16,256,128]{2,1,0:T(8,128)S(1)} %bitcast.7) | data formatting | bytes 4194304
  128.9 0.7 copy.7

commit v3 on v2

--- a/solution.py
+++ b/solution.py
@@ -16,22 +16,28 @@
 VMEM_LIMIT = 60817408
 FLOWS = (
     ("zz", 1, "xyx", 1),
+    ("zz", 3, "xyx", 3),
+    ("zz", 1, "xxy", 1),
     ("zz", 3, "xxy", 3),
     ("xx", 1, "yzz", 1),
     ("xx", 3, "yzz", 3),
 )
-UNITS = (8, 8, 8, 8)
+UNITS = (4, 4, 4, 4, 8, 8)
 DELAY = (
-    (6, 11, 14, 21, 26, 29),
-    (7, 8, 17, 20, 29, 59),
-    (5, 9, 12, 16, 26, 29),
-    (6, 9, 12, 16, 20, 32),
+    (1, 3, 9, 12, 16, 19),
+    (1, 4, 8, 10, 14, 18),
+    (2, 6, 10, 13, 15, 18),
+    (0, 8, 10, 13, 16, 19),
+    (1, 3, 5, 8, 11, 14),
+    (0, 3, 4, 7, 11, 14),
 )
 KEY = (
-    (20, 21, 22, 6, 0, 11),
-    (3, 17, 14, 19, 13, 5),
-    (23, 4, 8, 9, 2, 1),
-    (7, 15, 12, 10, 18, 16),
+    (10, 34, 32, 20, 2, 3),
+    (25, 19, 26, 16, 24, 17),
+    (21, 18, 0, 1, 15, 6),
+    (35, 7, 28, 13, 22, 33),
+    (5, 14, 8, 12, 27, 30),
+    (23, 4, 31, 29, 9, 11),
 )
 
 

time: 130 us -> 120 us (0.923)
  Pallas kernels: 127 us -> 118 us
    pallas_call x1, Pallas kernels: 127 us -> 118 us  [local(): pl.pallas_call(functools.partial(kernel, fit, root), out_shape=(pltpu.VME...]
where the time goes in v3:
time: 120 us
  Pallas kernels  118 us (98%)
  local copies, waits for them, and re-layouts  1.98 us (2%)
    pallas_call x1, Pallas kernels, local(): pl.pallas_call(functools.partial(kernel, fit, root), out_shape=(pltpu.VME...  118 us

profile of v3, /device:TPU:1, one launch (start us, length us, event | category | flops | bytes accessed | tf_op | source)
XLA Modules:
  0.0 120.4 jit_solution(12069934568116090041)
XLA Ops:
  0.6 117.7 %shard_map.41 = (f32[16,32,8,128]{3,2,1,0:T(8,128)S(1)}, f32[32,8,128]{2,1,0:T(8,128)S(1)}) custom-call(f32[384]{0:T(512)} %constant.2.clone.table_ref, f32[3,16,4,4,2,2,8,128]{7,6,5,4,3,2,1,0:T(8,128)} %bitcast.9), custom_call_target="tpu_custom_call" | custom-call | tf_op jit(solution)/shard_map/pallas_call | solution.py:396
  118.4 1.3 %copy.6 = f32[16,256,128]{2,1,0:T(8,128)} copy(f32[16,256,128]{2,1,0:T(8,128)S(1)} %bitcast.7) | data formatting | bytes 4194304
  119.7 0.7 copy.7

commit v4 on v2

--- a/solution.py
+++ b/solution.py
@@ -15,23 +15,29 @@
 STAGES = 6
 VMEM_LIMIT = 60817408
 FLOWS = (
-    ("zz", 1, "xyx", 1),
+    ("zz", 1, "xxy", 1),
     ("zz", 3, "xxy", 3),
+    ("zz", 1, "yxx", 1),
+    ("zz", 3, "yxx", 3),
     ("xx", 1, "yzz", 1),
     ("xx", 3, "yzz", 3),
 )
-UNITS = (8, 8, 8, 8)
+UNITS = (6, 6, 2, 2, 8, 8)
 DELAY = (
-    (6, 11, 14, 21, 26, 29),
-    (7, 8, 17, 20, 29, 59),
-    (5, 9, 12, 16, 26, 29),
-    (6, 9, 12, 16, 20, 32),
+    (1, 5, 8, 11, 14, 17),
+    (1, 6, 9, 11, 13, 16),
+    (1, 3, 5, 14, 17, 20),
+    (1, 5, 11, 15, 17, 20),
+    (0, 2, 4, 8, 11, 15),
+    (1, 3, 4, 8, 11, 15),
 )
 KEY = (
-    (20, 21, 22, 6, 0, 11),
-    (3, 17, 14, 19, 13, 5),
-    (23, 4, 8, 9, 2, 1),
-    (7, 15, 12, 10, 18, 16),
+    (31, 28, 16, 27, 9, 7),
+    (32, 23, 4, 5, 35, 11),
+    (12, 26, 29, 22, 18, 13),
+    (1, 14, 19, 8, 30, 10),
+    (21, 33, 24, 15, 20, 3),
+    (0, 6, 34, 17, 25, 2),
 )
 
 
@@ -87,7 +93,7 @@
 def flow_shapes(number):
     units = UNITS[number]
     rows = plan(FLOWS[number])
-    dims = {"own": (2, 3, 4, 2), "r1": (2, 3, 4, 2), "r2": (2, 3, 4, 2)}
+    dims = {"r1": (2, 2, 3, 4, 2), "r2": (2, 3, 4, 2)}
     dims["s0"] = (2, 2, 2, rows[0][1])
     blocks = (2, 2, 2)
     for at, (_, before, after, _, joins) in enumerate(rows):
@@ -99,7 +105,7 @@
     return {name: (units,) + dim + (8, 128) for name, dim in dims.items()}
 
 
-SEMS = ("ownl", "ownr", "r1", "r2", "r3", "r4", "r5")
+SEMS = ("r1", "r2", "r3", "r4", "r5")
 
 
 def scratch():
@@ -109,12 +115,14 @@
             shapes.append(pltpu.VMEM(shape, jnp.float32))
         for _ in SEMS:
             shapes.append(pltpu.SemaphoreType.DMA((UNITS[number],)))
-        shapes.append(pltpu.SemaphoreType.DMA((STAGES,)))
+    shapes.append(pltpu.SemaphoreType.DMA((STAGES,)))
+    shapes.append(pltpu.SMEM((TIMES * EXTRA,), jnp.float32))
+    shapes.append(pltpu.SemaphoreType.DMA(()))
     shapes.append(pltpu.SemaphoreType.DMA((2, 2)))
     return shapes
 
 
-def kernel(fit, root, table_ref, x_ref, coef_ref, var_ref, *refs):
+def kernel(fit, root, table_hbm, x_ref, coef_ref, var_ref, *refs):
     me = lax.axis_index("io")
     core = lax.rem(me, 2)
     y = lax.rem(lax.div(me, 2), 2)
@@ -127,6 +135,11 @@
 
     refs = list(refs)
     out_sem = refs.pop()
+    table_sem = refs.pop()
+    table_ref = refs.pop()
+    send = refs.pop()
+    table_copy = pltpu.make_async_copy(table_hbm, table_ref, table_sem)
+    table_copy.start()
     flows = []
     at, base = 0, 0
     for number, spec in enumerate(FLOWS):
@@ -141,8 +154,6 @@
         for name in SEMS:
             flow["sem"][name] = refs[at]
             at += 1
-        flow["send"] = refs[at]
-        at += 1
         flows.append(flow)
 
     def push(src, dst, send, recv, device):
@@ -189,23 +200,21 @@
                         src = x_ref.at[group, lat, :, block, :, half]
                     c = 1 - core if group == 1 else core
                     if not at_home:
-                        push(src, flow["r1"].at[i, slot, when], flow["send"].at[0], sem["r1"].at[i], dev(zz, xx, y, c))
+                        push(src, flow["r1"].at[i, 1, slot, when], send.at[0], sem["r1"].at[i], dev(zz, xx, y, c))
                     elif group == 1:
-                        push(src, flow["own"].at[i, slot, when], flow["send"].at[5], sem["ownr"].at[i], dev(zz, xx, y, c))
+                        push(src, flow["r1"].at[i, 0, slot, when], send.at[1], sem["r1"].at[i], dev(zz, xx, y, c))
                     else:
-                        pltpu.make_async_copy(src, flow["own"].at[i, slot, when], sem["ownl"].at[i]).start()
+                        pltpu.make_async_copy(src, flow["r1"].at[i, 0, slot, when], sem["r1"].at[i]).start()
 
     def second(flow, i):
         sem = flow["sem"]
-        await_bytes(flow["own"].at[i, :, 0:2], sem["ownl"].at[i])
-        await_bytes(flow["own"].at[i, :, 0], sem["ownr"].at[i])
         await_bytes(flow["r1"].at[i], sem["r1"].at[i])
         if flow["raw"] == "zz":
             to = dev(flip(z, flow["g"]), x, y, core)
         else:
             to = dev(z, flip(x, flow["g"]), y, core)
-        push(flow["own"].at[i, 1], flow["r2"].at[i, 0], flow["send"].at[1], sem["r2"].at[i], to)
-        push(flow["r1"].at[i, 1], flow["r2"].at[i, 1], flow["send"].at[1], sem["r2"].at[i], to)
+        push(flow["r1"].at[i, 0, 1], flow["r2"].at[i, 0], send.at[2], sem["r2"].at[i], to)
+        push(flow["r1"].at[i, 1, 1], flow["r2"].at[i, 1], send.at[2], sem["r2"].at[i], to)
 
     def partner(flow, stage):
         axis = flow["post"][stage]
@@ -218,7 +227,7 @@
 
     def send_stats(flow, i, stage, state):
         name = f"r{stage + 3}"
-        push(state.at[1], flow[name].at[i], flow["send"].at[stage + 2], flow["sem"][name].at[i], partner(flow, stage))
+        push(state.at[1], flow[name].at[i], send.at[stage + 3], flow["sem"][name].at[i], partner(flow, stage))
 
     def weights(chip, k):
         base = (chip * 3 + k) * EXTRA
@@ -226,7 +235,7 @@
 
     def reduce_raw(flow, i):
         await_bytes(flow["r2"].at[i], flow["sem"]["r2"].at[i])
-        own, r1, r2, s0 = flow["own"], flow["r1"], flow["r2"], flow["s0"]
+        r1, r2, s0 = flow["r1"], flow["r2"], flow["s0"]
         f, g, post = flow["f"], flow["g"], flow["post"]
         along_z = flow["raw"] == "zz"
         here = z if along_z else x
@@ -249,8 +258,8 @@
                     sums, moments, total = {}, [None] * EXTRA, None
                     for k in range(3):
                         values = (
-                            own[i, 0, k, block, lon_y],
-                            r1[i, 0, k, block, lon_y],
+                            r1[i, 0, 0, k, block, lon_y],
+                            r1[i, 1, 0, k, block, lon_y],
                             r2[i, 0, k, block, lon_y],
                             r2[i, 1, k, block, lon_y],
                         )
@@ -366,6 +375,10 @@
 
     @pl.loop(0, max(u + max(d) for u, d in zip(UNITS, DELAY)))
     def _(turn):
+        @pl.when(turn == min(d[2] for d in DELAY))
+        def _():
+            table_copy.wait()
+
         for _, number, stage in order:
             flow = flows[number]
             unit = turn - DELAY[number][stage]
@@ -374,13 +387,24 @@
             def _(flow=flow, stage=stage, unit=unit):
                 step(flow, stage, unit)
 
-    for flow in flows:
-        for stage in range(5):
-            await_bytes(flow[f"r{stage + 1}"], flow["send"].at[stage])
-        await_bytes(flow["own"].at[:, :, 0], flow["send"].at[5])
+    every = x_ref.reshape(3 * 16 * 64, 8, 128)
+    counts = [32 * 48, 32 * 16, 32 * 48]
+    for stage in range(3):
+        counts.append(sum(u * (4 >> stage) * f["rows"][stage][1] for u, f in zip(UNITS, flows)))
+    for kind, count in enumerate(counts):
+        await_bytes(every.at[pl.ds(0, count)], send.at[kind])
     for k in range(2):
         await_bytes(coef_ref.at[:, 0:16], out_sem.at[k, 0])
         await_bytes(var_ref.at[0:16], out_sem.at[k, 1])
+
+
+def store(coef_vmem, var_vmem, coef_ref, var_ref, sems):
+    copies = [pltpu.make_async_copy(coef_vmem.at[k], coef_ref.at[k], sems.at[k]) for k in range(HARM)]
+    copies.append(pltpu.make_async_copy(var_vmem, var_ref, sems.at[HARM]))
+    for copy in copies:
+        copy.start()
+    for copy in copies:
+        copy.wait()
 
 
 def local(snapshots):
@@ -393,13 +417,24 @@
             pltpu.VMEM((HARM, 32, 8, 128), jnp.float32),
             pltpu.VMEM((32, 8, 128), jnp.float32),
         ),
-        in_specs=[pl.BlockSpec(memory_space=pltpu.SMEM), pl.BlockSpec(memory_space=pl.ANY)],
+        in_specs=[pl.BlockSpec(memory_space=pl.ANY), pl.BlockSpec(memory_space=pl.ANY)],
         out_specs=(pl.BlockSpec(memory_space=pltpu.VMEM), pl.BlockSpec(memory_space=pltpu.VMEM)),
         scratch_shapes=scratch(),
         compiler_params=pltpu.CompilerParams(
             collective_id=0, has_side_effects=True, vmem_limit_bytes=VMEM_LIMIT
         ),
     )(jnp.asarray(table.reshape(-1), dtype=jnp.float32), tiles)
+    coeffs, variance = pl.pallas_call(
+        store,
+        out_shape=(
+            jax.ShapeDtypeStruct((HARM, 32, 8, 128), jnp.float32),
+            jax.ShapeDtypeStruct((32, 8, 128), jnp.float32),
+        ),
+        in_specs=[pl.BlockSpec(memory_space=pltpu.VMEM)] * 2,
+        out_specs=(pl.BlockSpec(memory_space=pl.ANY), pl.BlockSpec(memory_space=pl.ANY)),
+        scratch_shapes=[pltpu.SemaphoreType.DMA((HARM + 1,))],
+        compiler_params=pltpu.CompilerParams(vmem_limit_bytes=4 * 1024 * 1024),
+    )(coeffs, variance)
     return coeffs.reshape(HARM, 256, 128), variance.reshape(256, 128)
 
 

time: 130 us -> 118 us (0.908)
  Pallas kernels: 127 us -> 117 us
  local copies, waits for them, and re-layouts: 1.98 us -> 0 us
    pallas_call x1, Pallas kernels: 127 us -> 116 us  [local(): pl.pallas_call(functools.partial(kernel, fit, root), out_shape=(pltpu.VME...]
    unnamed x2 -> x0, local copies, waits for them, and re-layouts: 1.98 us -> none
    pallas_call x0 -> x1, Pallas kernels: none -> 1.49 us  [local(): pl.pallas_call(store, out_shape=(jax.ShapeDtypeStruct((HARM, 32, 8, 128),...]
where the time goes in v4:
time: 118 us
  Pallas kernels  117 us (99%)
    pallas_call x1, Pallas kernels, local(): pl.pallas_call(functools.partial(kernel, fit, root), out_shape=(pltpu.VME...  116 us

profile of v4, /device:TPU:1, one launch (start us, length us, event | category | flops | bytes accessed | tf_op | source)
XLA Modules:
  0.0 118.0 jit_solution(10667509463041355841)
XLA Ops:
  0.6 115.9 %shard_map.41 = (f32[16,32,8,128]{3,2,1,0:T(8,128)S(1)}, f32[32,8,128]{2,1,0:T(8,128)S(1)}) custom-call(f32[384]{0:T(512)} %constant.2.clone.table_hbm, f32[3,16,4,4,2,2,8,128]{7,6,5,4,3,2,1,0:T(8,128)} %bitcast.7), custom_call_target="tpu_custom_call" | custom-call | tf_op jit(solution)/shard_map/pallas_call | solution.py:414
  116.6 1.5 %shard_map.42 = (f32[16,32,8,128]{3,2,1,0:T(8,128)}, f32[32,8,128]{2,1,0:T(8,128)}) custom-call(f32[16,32,8,128]{3,2,1,0:T(8,128)S(1)} %get-tuple-element.6.coef_vmem, f32[32,8,128]{2,1,0:T(8,128)S(1)} %get-tuple-element.7.var_vmem), custom_call_target="tpu_custom_call" | custom-call | tf_op jit(solution)/shard_map/pallas_call | solution.py:427

commit v5 on v4

--- a/solution.py
+++ b/solution.py
@@ -24,20 +24,29 @@
 )
 UNITS = (6, 6, 2, 2, 8, 8)
 DELAY = (
-    (1, 5, 8, 11, 14, 17),
-    (1, 6, 9, 11, 13, 16),
-    (1, 3, 5, 14, 17, 20),
-    (1, 5, 11, 15, 17, 20),
-    (0, 2, 4, 8, 11, 15),
-    (1, 3, 4, 8, 11, 15),
+    (1, 5, 8, 10, 13, 16),
+    (0, 5, 7, 10, 13, 15),
+    (0, 2, 4, 12, 16, 20),
+    (4, 6, 8, 12, 15, 19),
+    (0, 3, 5, 7, 10, 14),
+    (0, 3, 4, 7, 10, 13),
+)
+POOL = (8, 2, 8, 6, 6, 2, 8, 8, 2, 2, 8, 8, 6, 6, 2)
+SEMS = (
+    (4, 13, 3, 4, 11),
+    (3, 12, 2, 12, 13),
+    (1, 5, 9, 8, 14),
+    (8, 14, 1, 5, 1),
+    (0, 6, 11, 7, 6),
+    (2, 7, 10, 0, 10),
 )
 KEY = (
-    (31, 28, 16, 27, 9, 7),
-    (32, 23, 4, 5, 35, 11),
-    (12, 26, 29, 22, 18, 13),
-    (1, 14, 19, 8, 30, 10),
-    (21, 33, 24, 15, 20, 3),
-    (0, 6, 34, 17, 25, 2),
+    (10, 25, 17, 14, 21, 16),
+    (20, 24, 28, 30, 0, 22),
+    (7, 18, 13, 35, 4, 12),
+    (9, 26, 32, 19, 31, 8),
+    (3, 1, 5, 34, 23, 15),
+    (11, 2, 27, 6, 29, 33),
 )
 
 
@@ -75,8 +84,8 @@
 
 def plan(flow):
     raw, _, post, _ = flow
-    merged = {"x"} if raw == "xx" else set()
-    values = 11 if raw == "xx" else 8
+    merged = {"zz": set(), "xx": {"x"}, "yxx": {"x", "y"}}[raw]
+    values = {"zz": 8, "xx": 11, "yxx": 17}[raw]
     rows = []
     for axis in post:
         joins = axis in ("x", "y") and axis not in merged
@@ -93,19 +102,24 @@
 def flow_shapes(number):
     units = UNITS[number]
     rows = plan(FLOWS[number])
-    dims = {"r1": (2, 2, 3, 4, 2), "r2": (2, 3, 4, 2)}
-    dims["s0"] = (2, 2, 2, rows[0][1])
-    blocks = (2, 2, 2)
+    if FLOWS[number][0] == "yxx":
+        dims = {"r1": (2, 3, 4, 4), "r2": (2, 2, 3, 4), "r3": (2, 2, 3, 4)}
+    else:
+        dims = {"r1": (2, 2, 3, 4, 2), "r2": (2, 3, 4, 2)}
+    blocks = (2,) * len(rows)
+    dims["s0"] = blocks + (rows[0][1],)
     for at, (_, before, after, _, joins) in enumerate(rows):
         blocks = blocks[1:]
-        dims[f"r{at + 3}"] = blocks + (before,)
+        dims[f"r{at + 6 - len(rows)}"] = blocks + (before,)
         if joins:
             dims[f"s{at + 1}"] = blocks + (after,)
     dims["out"] = (HARM + 1,)
     return {name: (units,) + dim + (8, 128) for name, dim in dims.items()}
 
 
-SEMS = ("r1", "r2", "r3", "r4", "r5")
+def sent_tiles(number):
+    rows = plan(FLOWS[number])
+    return [48] * (5 - len(rows)) + [before << (len(rows) - 1 - at) for at, (_, before, *_) in enumerate(rows)]
 
 
 def scratch():
@@ -113,8 +127,8 @@
     for number in range(len(FLOWS)):
         for shape in flow_shapes(number).values():
             shapes.append(pltpu.VMEM(shape, jnp.float32))
-        for _ in SEMS:
-            shapes.append(pltpu.SemaphoreType.DMA((UNITS[number],)))
+    for units in POOL:
+        shapes.append(pltpu.SemaphoreType.DMA((units,)))
     shapes.append(pltpu.SemaphoreType.DMA((STAGES,)))
     shapes.append(pltpu.SMEM((TIMES * EXTRA,), jnp.float32))
     shapes.append(pltpu.SemaphoreType.DMA(()))
@@ -150,11 +164,10 @@
         for name in flow_shapes(number):
             flow[name] = refs[at]
             at += 1
-        flow["sem"] = {}
-        for name in SEMS:
-            flow["sem"][name] = refs[at]
-            at += 1
+        flow["swap"] = flow["base"] % 2 == 0 and UNITS[number] % 2 == 0
         flows.append(flow)
+    for flow, pool in zip(flows, SEMS):
+        flow["sem"] = {f"r{k + 1}": refs[at + pool[k]] for k in range(5)}
 
     def push(src, dst, send, recv, device):
         pltpu.make_async_remote_copy(
@@ -179,12 +192,43 @@
         pl.semaphore_signal(barrier, inc=1, device_id={"io": friend}, device_id_type=pl.DeviceIdType.MESH)
     pl.semaphore_wait(barrier, len(friends))
 
-    def place(flow, i):
+    def place(flow, i, c):
         unit = flow["base"] + i
-        return lax.div(unit, 2), lax.rem(unit, 2)
+        half = lax.rem(i + 1 + c, 2) if flow["swap"] else lax.rem(unit, 2)
+        return lax.div(unit, 2), half
+
+    def begin_y(flow, i):
+        lat, half = place(flow, i, core)
+        _, half_other = place(flow, i, 1 - core)
+        for home, yy in ((1, 1 - y), (0, y)):
+            for group, when in ((0, core), (2, core + 1), (1, 2 * core)):
+                src = x_ref.at[group, lat, :, :, yy, half_other if group == 1 else half]
+                dst = flow["r1"].at[i, home, when]
+                recv = flow["sem"]["r1"].at[i]
+                c = 1 - core if group == 1 else core
+                if home:
+                    push(src, dst, send.at[0], recv, dev(z, x, yy, c))
+                elif group == 1:
+                    push(src, dst, send.at[1], recv, dev(z, x, yy, c))
+                else:
+                    pltpu.make_async_copy(src, dst, recv).start()
+
+    def second_y(flow, i):
+        await_bytes(flow["r1"].at[i], flow["sem"]["r1"].at[i])
+        to = flip(x, flow["f"])
+        for slot, block in ((1, flip(x, 2)), (0, to)):
+            push(flow["r1"].at[i, :, :, :, block], flow["r2"].at[i, slot], send.at[2], flow["sem"]["r2"].at[i], dev(z, to, y, core))
+
+    def third_y(flow, i):
+        await_bytes(flow["r2"].at[i], flow["sem"]["r2"].at[i])
+        to = flip(x, flow["g"])
+        device = dev(z, to, y, core)
+        push(flow["r1"].at[i, :, :, :, to], flow["r3"].at[i, 0], send.at[3], flow["sem"]["r3"].at[i], device)
+        push(flow["r2"].at[i, 1], flow["r3"].at[i, 1], send.at[3], flow["sem"]["r3"].at[i], device)
 
     def begin(flow, i):
-        lat, half = place(flow, i)
+        lat, half = place(flow, i, core)
+        _, half_other = place(flow, i, 1 - core)
         sem = flow["sem"]
         along_z = flow["raw"] == "zz"
         here = z if along_z else x
@@ -194,10 +238,11 @@
             zz, xx = (spot, x) if along_z else (z, spot)
             for slot, block in ((0, spot), (1, flip(spot, flow["g"]))):
                 for group, when in ((0, core), (2, core + 1), (1, 2 * core)):
+                    lon = half_other if group == 1 else half
                     if along_z:
-                        src = x_ref.at[group, lat, block, :, :, half]
+                        src = x_ref.at[group, lat, block, :, :, lon]
                     else:
-                        src = x_ref.at[group, lat, :, block, :, half]
+                        src = x_ref.at[group, lat, :, block, :, lon]
                     c = 1 - core if group == 1 else core
                     if not at_home:
                         push(src, flow["r1"].at[i, 1, slot, when], send.at[0], sem["r1"].at[i], dev(zz, xx, y, c))
@@ -226,12 +271,51 @@
         return dev(flip(z, mask), x, y, core)
 
     def send_stats(flow, i, stage, state):
-        name = f"r{stage + 3}"
-        push(state.at[1], flow[name].at[i], send.at[stage + 3], flow["sem"][name].at[i], partner(flow, stage))
+        step = stage + 6 - len(flow["rows"])
+        name = f"r{step}"
+        push(state.at[1], flow[name].at[i], send.at[step], flow["sem"][name].at[i], partner(flow, stage))
 
     def weights(chip, k):
         base = (chip * 3 + k) * EXTRA
         return [table_ref[base + j] for j in range(EXTRA)]
+
+    def fold(pieces):
+        sums, moments, total = {}, [None] * EXTRA, None
+        for kind, k, value, chip in pieces:
+            key = (kind, k)
+            sums[key] = value if key not in sums else sums[key] + value
+            w = weights(chip, k)
+            for j in range(EXTRA):
+                term = w[j] * value
+                moments[j] = term if moments[j] is None else moments[j] + term
+            square = value * value
+            total = square if total is None else total + square
+        return sums, moments, total
+
+    def reduce_y(flow, i):
+        await_bytes(flow["r3"].at[i], flow["sem"]["r3"].at[i])
+        r1, r2, r3, s0 = flow["r1"], flow["r2"], flow["r3"], flow["s0"]
+        spots = (x, flip(x, flow["f"]), flip(x, flow["g"]), flip(x, 2))
+        for b0 in (1, 0):
+            for b1 in range(2):
+                lon = (b0 * flow["pf"]) ^ (b1 * flow["pg"])
+                block = z if lon == 0 else flip(z, lon)
+                pieces = []
+                for k in range(3):
+                    for b, yy in enumerate((y, 1 - y)):
+                        values = (r1[i, b, k, block, x], r2[i, 0, b, k, block], r3[i, 0, b, k, block], r3[i, 1, b, k, block])
+                        for number, value in enumerate(values):
+                            a = 0 if number in (0, 3) else 1
+                            pieces.append(((a, b), k, value, z * 8 + spots[number] * 2 + yy))
+                sums, moments, total = fold(pieces)
+                for ((a, b), k), value in sums.items():
+                    xl = 1 - parity if a else parity
+                    yy = 1 - y if b else y
+                    s0[i, b0, b1, 3 * (2 * xl + yy) + k] = value
+                for j in range(EXTRA):
+                    s0[i, b0, b1, MONTHS + j] = moments[j]
+                s0[i, b0, b1, MONTHS + EXTRA] = total
+        send_stats(flow, i, 0, s0.at[i])
 
     def reduce_raw(flow, i):
         await_bytes(flow["r2"].at[i], flow["sem"]["r2"].at[i])
@@ -255,7 +339,7 @@
                             lon = lon ^ (bit * (flow["pg"] if seen else flow["pf"]))
                             seen = True
                     block = across if lon == 0 else flip(across, lon)
-                    sums, moments, total = {}, [None] * EXTRA, None
+                    pieces = []
                     for k in range(3):
                         values = (
                             r1[i, 0, 0, k, block, lon_y],
@@ -264,14 +348,9 @@
                             r2[i, 1, k, block, lon_y],
                         )
                         for number, value in enumerate(values):
-                            key = (0 if along_z or number in (0, 3) else 1, k)
-                            sums[key] = value if key not in sums else sums[key] + value
-                            w = weights(chips[number], k)
-                            for j in range(EXTRA):
-                                term = w[j] * value
-                                moments[j] = term if moments[j] is None else moments[j] + term
-                            square = value * value
-                            total = square if total is None else total + square
+                            kind = 0 if along_z or number in (0, 3) else 1
+                            pieces.append((kind, k, value, chips[number]))
+                    sums, moments, total = fold(pieces)
                     for (a, k), value in sums.items():
                         if along_z:
                             s0[i, b0, b1, b2, k] = value
@@ -284,13 +363,13 @@
         send_stats(flow, i, 0, s0.at[i])
 
     def merge(flow, i, stage):
-        name = f"r{stage + 3}"
+        name = f"r{stage + 6 - len(flow['rows'])}"
         await_bytes(flow[name].at[i], flow["sem"][name].at[i])
         axis, before, after, merged, joins = flow["rows"][stage]
         theirs = flow[name].at[i]
         mine = flow["state"].at[0]
         blocks = [()]
-        for _ in range(2 - stage):
+        for _ in range(len(flow["rows"]) - 1 - stage):
             blocks = [b + (bit,) for b in blocks for bit in (1, 0)]
         if not joins:
             for b in blocks:
@@ -319,12 +398,12 @@
             joins = flow["rows"][done][4]
             flow["state"] = flow[f"s{done + 1}"].at[i] if joins else flow["state"].at[0]
         state = merge(flow, i, stage - 1)
-        if stage < 3:
+        if stage < len(flow["rows"]):
             send_stats(flow, i, stage, state)
         return state
 
     def finish(flow, i):
-        state = exchange(flow, i, 3)
+        state = exchange(flow, i, len(flow["rows"]))
         out = flow["out"]
         w = [state[j] for j in range(MONTHS + EXTRA)]
         total = state[MONTHS + EXTRA]
@@ -344,7 +423,7 @@
                 value = term if value is None else value + term
             explained = value * value if explained is None else explained + value * value
         out[i, HARM] = (total - explained) * (1.0 / TIMES)
-        lat, half = place(flow, i)
+        lat, half = place(flow, i, core)
         row = core * 16 + lat
 
         @pl.when(half != core)
@@ -360,22 +439,21 @@
             var_ref[row] = out[i, HARM]
 
     def step(flow, stage, i):
-        if stage == 0:
-            begin(flow, i)
-        elif stage == 1:
-            second(flow, i)
-        elif stage == 2:
-            reduce_raw(flow, i)
+        early = (begin, second, reduce_raw)
+        if flow["raw"] == "yxx":
+            early = (begin_y, second_y, third_y, reduce_y)
+        if stage < len(early):
+            early[stage](flow, i)
         elif stage == 5:
             finish(flow, i)
         else:
-            exchange(flow, i, stage - 2)
+            exchange(flow, i, stage + 1 - len(early))
 
     order = sorted((KEY[f][s], f, s) for f in range(len(FLOWS)) for s in range(STAGES))
 
     @pl.loop(0, max(u + max(d) for u, d in zip(UNITS, DELAY)))
     def _(turn):
-        @pl.when(turn == min(d[2] for d in DELAY))
+        @pl.when(turn == min(d[5 - len(f["rows"])] for d, f in zip(DELAY, flows)))
         def _():
             table_copy.wait()
 
@@ -388,9 +466,8 @@
                 step(flow, stage, unit)
 
     every = x_ref.reshape(3 * 16 * 64, 8, 128)
-    counts = [32 * 48, 32 * 16, 32 * 48]
-    for stage in range(3):
-        counts.append(sum(u * (4 >> stage) * f["rows"][stage][1] for u, f in zip(UNITS, flows)))
+    totals = [sum(u * sent_tiles(n)[k] for n, u in enumerate(UNITS)) for k in range(5)]
+    counts = [totals[0], 32 * 16] + totals[1:]
     for kind, count in enumerate(counts):
         await_bytes(every.at[pl.ds(0, count)], send.at[kind])
     for k in range(2):

time: 118 us -> 116 us (0.983)
    pallas_call x1, Pallas kernels: 116 us -> 114 us  [local(): pl.pallas_call(functools.partial(kernel, fit, root), out_shape=(pltpu.VME...]
where the time goes in v5:
time: 116 us
  Pallas kernels  116 us (100%)
    pallas_call x1, Pallas kernels, local(): pl.pallas_call(functools.partial(kernel, fit, root), out_shape=(pltpu.VME...  114 us

profile of v5, /device:TPU:1, one launch (start us, length us, event | category | flops | bytes accessed | tf_op | source)
XLA Modules:
  0.0 116.2 jit_solution(13714265230760842570)
XLA Ops:
  0.6 114.0 %shard_map.41 = (f32[16,32,8,128]{3,2,1,0:T(8,128)S(1)}, f32[32,8,128]{2,1,0:T(8,128)S(1)}) custom-call(f32[384]{0:T(512)} %constant.2.clone.table_hbm, f32[3,16,4,4,2,2,8,128]{7,6,5,4,3,2,1,0:T(8,128)} %bitcast.7), custom_call_target="tpu_custom_call" | custom-call | tf_op jit(solution)/shard_map/pallas_call | solution.py:491
  114.7 1.5 %shard_map.42 = (f32[16,32,8,128]{3,2,1,0:T(8,128)}, f32[32,8,128]{2,1,0:T(8,128)}) custom-call(f32[16,32,8,128]{3,2,1,0:T(8,128)S(1)} %get-tuple-element.6.coef_vmem, f32[32,8,128]{2,1,0:T(8,128)S(1)} %get-tuple-element.7.var_vmem), custom_call_target="tpu_custom_call" | custom-call | tf_op jit(solution)/shard_map/pallas_call | solution.py:504

commit v6 on v5

--- a/solution.py
+++ b/solution.py
@@ -15,38 +15,54 @@
 STAGES = 6
 VMEM_LIMIT = 60817408
 FLOWS = (
-    ("zz", 1, "xxy", 1),
-    ("zz", 3, "xxy", 3),
+    ("zz", 3, "xyx", 3),
+    ("zz", 1, "xyx", 1),
+    ("xx", 1, "zzy", 1),
+    ("xx", 3, "zzy", 3),
+    ("xx", 1, "yzz", 1),
+    ("xx", 3, "yzz", 3),
     ("zz", 1, "yxx", 1),
     ("zz", 3, "yxx", 3),
-    ("xx", 1, "yzz", 1),
-    ("xx", 3, "yzz", 3),
+    ("yxx", 1, "zz", 1),
+    ("yxx", 3, "zz", 3),
 )
-UNITS = (6, 6, 2, 2, 8, 8)
+UNITS = (2, 2, 2, 2, 4, 4, 5, 5, 3, 3)
 DELAY = (
-    (1, 5, 8, 10, 13, 16),
-    (0, 5, 7, 10, 13, 15),
-    (0, 2, 4, 12, 16, 20),
-    (4, 6, 8, 12, 15, 19),
-    (0, 3, 5, 7, 10, 14),
-    (0, 3, 4, 7, 10, 13),
+    (4, 7, 9, 14, 17, 20),
+    (3, 7, 10, 13, 16, 20),
+    (3, 7, 9, 10, 16, 19),
+    (0, 5, 7, 10, 12, 15),
+    (0, 4, 5, 7, 14, 18),
+    (2, 4, 5, 8, 14, 18),
+    (0, 3, 6, 9, 13, 17),
+    (0, 4, 6, 10, 13, 17),
+    (1, 7, 9, 11, 15, 19),
+    (1, 6, 7, 9, 14, 18),
 )
-POOL = (8, 2, 8, 6, 6, 2, 8, 8, 2, 2, 8, 8, 6, 6, 2)
+POOL = (5, 5, 5, 5, 5, 5, 4, 4, 4, 4, 4, 4, 3, 3, 2, 2, 2, 2, 2, 2, 2, 2, 2, 2)
 SEMS = (
-    (4, 13, 3, 4, 11),
-    (3, 12, 2, 12, 13),
-    (1, 5, 9, 8, 14),
-    (8, 14, 1, 5, 1),
-    (0, 6, 11, 7, 6),
-    (2, 7, 10, 0, 10),
+    ((17, 2), (20, 2), (16, 2), (23, 2), (12, 2)),
+    ((15, 2), (22, 2), (12, 2), (15, 2), (14, 2)),
+    ((16, 2), (19, 2), (14, 2), (18, 2), (21, 2)),
+    ((14, 2), (18, 2), (21, 2), (17, 2), (19, 2)),
+    ((6, 4), (8, 4), (10, 4), (1, 4), (9, 4)),
+    ((7, 4), (9, 4), (11, 4), (6, 4), (7, 4)),
+    ((1, 5), (2, 5), (4, 5), (2, 5), (0, 5)),
+    ((0, 5), (3, 5), (5, 5), (3, 5), (4, 5)),
+    ((12, 3), (7, 3), (13, 3), (10, 3), (11, 3)),
+    ((13, 3), (0, 3), (9, 3), (8, 3), (5, 3)),
 )
 KEY = (
-    (10, 25, 17, 14, 21, 16),
-    (20, 24, 28, 30, 0, 22),
-    (7, 18, 13, 35, 4, 12),
-    (9, 26, 32, 19, 31, 8),
-    (3, 1, 5, 34, 23, 15),
-    (11, 2, 27, 6, 29, 33),
+    (25, 44, 55, 12, 14, 9),
+    (38, 56, 19, 17, 34, 40),
+    (50, 29, 16, 30, 27, 7),
+    (10, 45, 52, 15, 47, 20),
+    (58, 11, 36, 23, 57, 43),
+    (21, 22, 42, 49, 3, 13),
+    (51, 24, 18, 46, 28, 8),
+    (1, 0, 41, 26, 54, 4),
+    (31, 32, 5, 33, 35, 6),
+    (37, 2, 59, 48, 39, 53),
 )
 
 
@@ -167,7 +183,11 @@
         flow["swap"] = flow["base"] % 2 == 0 and UNITS[number] % 2 == 0
         flows.append(flow)
     for flow, pool in zip(flows, SEMS):
-        flow["sem"] = {f"r{k + 1}": refs[at + pool[k]] for k in range(5)}
+        flow["sem"] = {f"r{k + 1}": (refs[at + pool[k][0]], pool[k][1]) for k in range(5)}
+
+    def arrival(flow, name, i):
+        ref, length = flow["sem"][name]
+        return ref.at[i if length == flow["units"] else lax.rem(i, length)]
 
     def push(src, dst, send, recv, device):
         pltpu.make_async_remote_copy(
@@ -183,7 +203,7 @@
         pltpu.make_async_copy(ref, ref, sem).wait()
 
     barrier = pltpu.get_barrier_semaphore()
-    friends = [dev(z, x, y, 1 - core), dev(z, x, 1 - y, core)]
+    friends = [dev(z, x, y, 1 - core), dev(z, x, 1 - y, core), dev(z, x, 1 - y, 1 - core)]
     for mask in (1, 3):
         for c in (core, 1 - core):
             friends.append(dev(flip(z, mask), x, y, c))
@@ -204,7 +224,7 @@
             for group, when in ((0, core), (2, core + 1), (1, 2 * core)):
                 src = x_ref.at[group, lat, :, :, yy, half_other if group == 1 else half]
                 dst = flow["r1"].at[i, home, when]
-                recv = flow["sem"]["r1"].at[i]
+                recv = arrival(flow, "r1", i)
                 c = 1 - core if group == 1 else core
                 if home:
                     push(src, dst, send.at[0], recv, dev(z, x, yy, c))
@@ -214,22 +234,21 @@
                     pltpu.make_async_copy(src, dst, recv).start()
 
     def second_y(flow, i):
-        await_bytes(flow["r1"].at[i], flow["sem"]["r1"].at[i])
+        await_bytes(flow["r1"].at[i], arrival(flow, "r1", i))
         to = flip(x, flow["f"])
         for slot, block in ((1, flip(x, 2)), (0, to)):
-            push(flow["r1"].at[i, :, :, :, block], flow["r2"].at[i, slot], send.at[2], flow["sem"]["r2"].at[i], dev(z, to, y, core))
+            push(flow["r1"].at[i, :, :, :, block], flow["r2"].at[i, slot], send.at[2], arrival(flow, "r2", i), dev(z, to, y, core))
 
     def third_y(flow, i):
-        await_bytes(flow["r2"].at[i], flow["sem"]["r2"].at[i])
+        await_bytes(flow["r2"].at[i], arrival(flow, "r2", i))
         to = flip(x, flow["g"])
         device = dev(z, to, y, core)
-        push(flow["r1"].at[i, :, :, :, to], flow["r3"].at[i, 0], send.at[3], flow["sem"]["r3"].at[i], device)
-        push(flow["r2"].at[i, 1], flow["r3"].at[i, 1], send.at[3], flow["sem"]["r3"].at[i], device)
+        push(flow["r1"].at[i, :, :, :, to], flow["r3"].at[i, 0], send.at[3], arrival(flow, "r3", i), device)
+        push(flow["r2"].at[i, 1], flow["r3"].at[i, 1], send.at[3], arrival(flow, "r3", i), device)
 
     def begin(flow, i):
         lat, half = place(flow, i, core)
         _, half_other = place(flow, i, 1 - core)
-        sem = flow["sem"]
         along_z = flow["raw"] == "zz"
         here = z if along_z else x
         there = flip(here, flow["f"])
@@ -245,21 +264,20 @@
                         src = x_ref.at[group, lat, :, block, :, lon]
                     c = 1 - core if group == 1 else core
                     if not at_home:
-                        push(src, flow["r1"].at[i, 1, slot, when], send.at[0], sem["r1"].at[i], dev(zz, xx, y, c))
+                        push(src, flow["r1"].at[i, 1, slot, when], send.at[0], arrival(flow, "r1", i), dev(zz, xx, y, c))
                     elif group == 1:
-                        push(src, flow["r1"].at[i, 0, slot, when], send.at[1], sem["r1"].at[i], dev(zz, xx, y, c))
+                        push(src, flow["r1"].at[i, 0, slot, when], send.at[1], arrival(flow, "r1", i), dev(zz, xx, y, c))
                     else:
-                        pltpu.make_async_copy(src, flow["r1"].at[i, 0, slot, when], sem["r1"].at[i]).start()
+                        pltpu.make_async_copy(src, flow["r1"].at[i, 0, slot, when], arrival(flow, "r1", i)).start()
 
     def second(flow, i):
-        sem = flow["sem"]
-        await_bytes(flow["r1"].at[i], sem["r1"].at[i])
+        await_bytes(flow["r1"].at[i], arrival(flow, "r1", i))
         if flow["raw"] == "zz":
             to = dev(flip(z, flow["g"]), x, y, core)
         else:
             to = dev(z, flip(x, flow["g"]), y, core)
-        push(flow["r1"].at[i, 0, 1], flow["r2"].at[i, 0], send.at[2], sem["r2"].at[i], to)
-        push(flow["r1"].at[i, 1, 1], flow["r2"].at[i, 1], send.at[2], sem["r2"].at[i], to)
+        push(flow["r1"].at[i, 0, 1], flow["r2"].at[i, 0], send.at[2], arrival(flow, "r2", i), to)
+        push(flow["r1"].at[i, 1, 1], flow["r2"].at[i, 1], send.at[2], arrival(flow, "r2", i), to)
 
     def partner(flow, stage):
         axis = flow["post"][stage]
@@ -273,7 +291,7 @@
     def send_stats(flow, i, stage, state):
         step = stage + 6 - len(flow["rows"])
         name = f"r{step}"
-        push(state.at[1], flow[name].at[i], send.at[step], flow["sem"][name].at[i], partner(flow, stage))
+        push(state.at[1], flow[name].at[i], send.at[step], arrival(flow, name, i), partner(flow, stage))
 
     def weights(chip, k):
         base = (chip * 3 + k) * EXTRA
@@ -293,7 +311,7 @@
         return sums, moments, total
 
     def reduce_y(flow, i):
-        await_bytes(flow["r3"].at[i], flow["sem"]["r3"].at[i])
+        await_bytes(flow["r3"].at[i], arrival(flow, "r3", i))
         r1, r2, r3, s0 = flow["r1"], flow["r2"], flow["r3"], flow["s0"]
         spots = (x, flip(x, flow["f"]), flip(x, flow["g"]), flip(x, 2))
         for b0 in (1, 0):
@@ -318,7 +336,7 @@
         send_stats(flow, i, 0, s0.at[i])
 
     def reduce_raw(flow, i):
-        await_bytes(flow["r2"].at[i], flow["sem"]["r2"].at[i])
+        await_bytes(flow["r2"].at[i], arrival(flow, "r2", i))
         r1, r2, s0 = flow["r1"], flow["r2"], flow["s0"]
         f, g, post = flow["f"], flow["g"], flow["post"]
         along_z = flow["raw"] == "zz"
@@ -364,7 +382,7 @@
 
     def merge(flow, i, stage):
         name = f"r{stage + 6 - len(flow['rows'])}"
-        await_bytes(flow[name].at[i], flow["sem"][name].at[i])
+        await_bytes(flow[name].at[i], arrival(flow, name, i))
         axis, before, after, merged, joins = flow["rows"][stage]
         theirs = flow[name].at[i]
         mine = flow["state"].at[0]

time: 116 us -> 114 us (0.983)
  Pallas kernels: 116 us -> 113 us
    pallas_call x1, Pallas kernels: 114 us -> 112 us  [local(): pl.pallas_call(functools.partial(kernel, fit, root), out_shape=(pltpu.VME...]
where the time goes in v6:
time: 114 us
  Pallas kernels  113 us (99%)
    pallas_call x1, Pallas kernels, local(): pl.pallas_call(functools.partial(kernel, fit, root), out_shape=(pltpu.VME...  112 us

profile of v6, /device:TPU:1, one launch (start us, length us, event | category | flops | bytes accessed | tf_op | source)
XLA Modules:
  0.0 113.8 jit_solution(18364167332618807797)
XLA Ops:
  0.6 111.7 %shard_map.41 = (f32[16,32,8,128]{3,2,1,0:T(8,128)S(1)}, f32[32,8,128]{2,1,0:T(8,128)S(1)}) custom-call(f32[384]{0:T(512)} %constant.2.clone.table_hbm, f32[3,16,4,4,2,2,8,128]{7,6,5,4,3,2,1,0:T(8,128)} %bitcast.7), custom_call_target="tpu_custom_call" | custom-call | tf_op jit(solution)/shard_map/pallas_call | solution.py:509
  112.4 1.5 %shard_map.42 = (f32[16,32,8,128]{3,2,1,0:T(8,128)}, f32[32,8,128]{2,1,0:T(8,128)}) custom-call(f32[16,32,8,128]{3,2,1,0:T(8,128)S(1)} %get-tuple-element.6.coef_vmem, f32[32,8,128]{2,1,0:T(8,128)S(1)} %get-tuple-element.7.var_vmem), custom_call_target="tpu_custom_call" | custom-call | tf_op jit(solution)/shard_map/pallas_call | solution.py:522

commit v7 on v6

--- a/solution.py
+++ b/solution.py
@@ -39,18 +39,19 @@
     (1, 7, 9, 11, 15, 19),
     (1, 6, 7, 9, 14, 18),
 )
+FIRST = (7, 3, 6, 4, 8)
 POOL = (5, 5, 5, 5, 5, 5, 4, 4, 4, 4, 4, 4, 3, 3, 2, 2, 2, 2, 2, 2, 2, 2, 2, 2)
 SEMS = (
-    ((17, 2), (20, 2), (16, 2), (23, 2), (12, 2)),
-    ((15, 2), (22, 2), (12, 2), (15, 2), (14, 2)),
-    ((16, 2), (19, 2), (14, 2), (18, 2), (21, 2)),
-    ((14, 2), (18, 2), (21, 2), (17, 2), (19, 2)),
-    ((6, 4), (8, 4), (10, 4), (1, 4), (9, 4)),
-    ((7, 4), (9, 4), (11, 4), (6, 4), (7, 4)),
-    ((1, 5), (2, 5), (4, 5), (2, 5), (0, 5)),
-    ((0, 5), (3, 5), (5, 5), (3, 5), (4, 5)),
-    ((12, 3), (7, 3), (13, 3), (10, 3), (11, 3)),
-    ((13, 3), (0, 3), (9, 3), (8, 3), (5, 3)),
+    ((15, 2), (18, 2), (8, 2), (20, 2), (3, 2)),
+    ((17, 2), (19, 2), (16, 2), (21, 2), (14, 2)),
+    ((16, 2), (20, 2), (14, 2), (17, 2), (22, 2)),
+    ((14, 2), (21, 2), (22, 2), (23, 2), (15, 2)),
+    ((6, 4), (9, 4), (8, 4), (1, 4), (7, 4)),
+    ((7, 4), (10, 4), (11, 4), (6, 4), (11, 4)),
+    ((0, 5), (2, 5), (4, 5), (2, 5), (0, 5)),
+    ((1, 5), (3, 5), (5, 5), (3, 5), (4, 5)),
+    ((12, 3), (7, 3), (13, 3), (12, 3), (9, 3)),
+    ((13, 3), (0, 3), (9, 3), (10, 3), (5, 3)),
 )
 KEY = (
     (25, 44, 55, 12, 14, 9),
@@ -130,7 +131,10 @@
         if joins:
             dims[f"s{at + 1}"] = blocks + (after,)
     dims["out"] = (HARM + 1,)
-    return {name: (units,) + dim + (8, 128) for name, dim in dims.items()}
+    shapes = {name: (units,) + dim + (8, 128) for name, dim in dims.items()}
+    if number in FIRST:
+        shapes["stage"] = ((3, 4, 4) if FLOWS[number][0] == "yxx" else (2, 3, 4, 2)) + (8, 128)
+    return shapes
 
 
 def sent_tiles(number):
@@ -148,6 +152,7 @@
     shapes.append(pltpu.SemaphoreType.DMA((STAGES,)))
     shapes.append(pltpu.SMEM((TIMES * EXTRA,), jnp.float32))
     shapes.append(pltpu.SemaphoreType.DMA(()))
+    shapes.append(pltpu.SemaphoreType.DMA(()))
     shapes.append(pltpu.SemaphoreType.DMA((2, 2)))
     return shapes
 
@@ -165,6 +170,7 @@
 
     refs = list(refs)
     out_sem = refs.pop()
+    stage_sem = refs.pop()
     table_sem = refs.pop()
     table_ref = refs.pop()
     send = refs.pop()
@@ -210,14 +216,13 @@
             friends.append(dev(z, flip(x, mask), y, c))
     for friend in friends:
         pl.semaphore_signal(barrier, inc=1, device_id={"io": friend}, device_id_type=pl.DeviceIdType.MESH)
-    pl.semaphore_wait(barrier, len(friends))
 
     def place(flow, i, c):
         unit = flow["base"] + i
         half = lax.rem(i + 1 + c, 2) if flow["swap"] else lax.rem(unit, 2)
         return lax.div(unit, 2), half
 
-    def begin_y(flow, i):
+    def begin_y(flow, i, mode=None):
         lat, half = place(flow, i, core)
         _, half_other = place(flow, i, 1 - core)
         for home, yy in ((1, 1 - y), (0, y)):
@@ -226,7 +231,12 @@
                 dst = flow["r1"].at[i, home, when]
                 recv = arrival(flow, "r1", i)
                 c = 1 - core if group == 1 else core
-                if home:
+                if mode == "fetch":
+                    if home:
+                        pltpu.make_async_copy(src, flow["stage"].at[group], stage_sem).start()
+                elif home:
+                    if mode == "staged":
+                        src = flow["stage"].at[group]
                     push(src, dst, send.at[0], recv, dev(z, x, yy, c))
                 elif group == 1:
                     push(src, dst, send.at[1], recv, dev(z, x, yy, c))
@@ -246,7 +256,7 @@
         push(flow["r1"].at[i, :, :, :, to], flow["r3"].at[i, 0], send.at[3], arrival(flow, "r3", i), device)
         push(flow["r2"].at[i, 1], flow["r3"].at[i, 1], send.at[3], arrival(flow, "r3", i), device)
 
-    def begin(flow, i):
+    def begin(flow, i, mode=None):
         lat, half = place(flow, i, core)
         _, half_other = place(flow, i, 1 - core)
         along_z = flow["raw"] == "zz"
@@ -263,7 +273,12 @@
                     else:
                         src = x_ref.at[group, lat, :, block, :, lon]
                     c = 1 - core if group == 1 else core
-                    if not at_home:
+                    if mode == "fetch":
+                        if not at_home:
+                            pltpu.make_async_copy(src, flow["stage"].at[slot, group], stage_sem).start()
+                    elif not at_home:
+                        if mode == "staged":
+                            src = flow["stage"].at[slot, group]
                         push(src, flow["r1"].at[i, 1, slot, when], send.at[0], arrival(flow, "r1", i), dev(zz, xx, y, c))
                     elif group == 1:
                         push(src, flow["r1"].at[i, 0, slot, when], send.at[1], arrival(flow, "r1", i), dev(zz, xx, y, c))
@@ -467,6 +482,17 @@
         else:
             exchange(flow, i, stage + 1 - len(early))
 
+    every = x_ref.reshape(3 * 16 * 64, 8, 128)
+
+    def start(mode):
+        for number in FIRST:
+            (begin_y if flows[number]["raw"] == "yxx" else begin)(flows[number], core * 0, mode)
+
+    start("fetch")
+    pl.semaphore_wait(barrier, len(friends))
+    await_bytes(every.at[pl.ds(0, 48 * len(FIRST))], stage_sem)
+    start("staged")
+
     order = sorted((KEY[f][s], f, s) for f in range(len(FLOWS)) for s in range(STAGES))
 
     @pl.loop(0, max(u + max(d) for u, d in zip(UNITS, DELAY)))
@@ -479,11 +505,12 @@
             flow = flows[number]
             unit = turn - DELAY[number][stage]
 
-            @pl.when((unit >= 0) & (unit < flow["units"]))
+            lowest = 1 if stage == 0 and number in FIRST else 0
+
+            @pl.when((unit >= lowest) & (unit < flow["units"]))
             def _(flow=flow, stage=stage, unit=unit):
                 step(flow, stage, unit)
 
-    every = x_ref.reshape(3 * 16 * 64, 8, 128)
     totals = [sum(u * sent_tiles(n)[k] for n, u in enumerate(UNITS)) for k in range(5)]
     counts = [totals[0], 32 * 16] + totals[1:]
     for kind, count in enumerate(counts):

time: 114 us -> 114 us (level)
  no operation moved by 1% of the time
where the time goes in v7:
time: 114 us
  Pallas kernels  113 us (99%)
    pallas_call x1, Pallas kernels, local(): pl.pallas_call(functools.partial(kernel, fit, root), out_shape=(pltpu.VME...  112 us

profile of v7, /device:TPU:1, one launch (start us, length us, event | category | flops | bytes accessed | tf_op | source)
XLA Modules:
  0.0 113.7 jit_solution(9031530361299009374)
XLA Ops:
  0.6 111.5 %shard_map.41 = (f32[16,32,8,128]{3,2,1,0:T(8,128)S(1)}, f32[32,8,128]{2,1,0:T(8,128)S(1)}) custom-call(f32[384]{0:T(512)} %constant.2.clone.table_hbm, f32[3,16,4,4,2,2,8,128]{7,6,5,4,3,2,1,0:T(8,128)} %bitcast.7), custom_call_target="tpu_custom_call" | custom-call | tf_op jit(solution)/shard_map/pallas_call | solution.py:536
  112.2 1.5 %shard_map.42 = (f32[16,32,8,128]{3,2,1,0:T(8,128)}, f32[32,8,128]{2,1,0:T(8,128)}) custom-call(f32[16,32,8,128]{3,2,1,0:T(8,128)S(1)} %get-tuple-element.6.coef_vmem, f32[32,8,128]{2,1,0:T(8,128)S(1)} %get-tuple-element.7.var_vmem), custom_call_target="tpu_custom_call" | custom-call | tf_op jit(solution)/shard_map/pallas_call | solution.py:549

commit v8 on v7

--- a/solution.py
+++ b/solution.py
@@ -210,11 +210,11 @@
 
     barrier = pltpu.get_barrier_semaphore()
     friends = [dev(z, x, y, 1 - core), dev(z, x, 1 - y, core), dev(z, x, 1 - y, 1 - core)]
-    for mask in (1, 3):
+    for mask in (3, 1):
         for c in (core, 1 - core):
             friends.append(dev(flip(z, mask), x, y, c))
             friends.append(dev(z, flip(x, mask), y, c))
-    for friend in friends:
+    for friend in friends[3:] + friends[:3]:
         pl.semaphore_signal(barrier, inc=1, device_id={"io": friend}, device_id_type=pl.DeviceIdType.MESH)
 
     def place(flow, i, c):
@@ -521,8 +521,10 @@
 
 
 def store(coef_vmem, var_vmem, coef_ref, var_ref, sems):
-    copies = [pltpu.make_async_copy(coef_vmem.at[k], coef_ref.at[k], sems.at[k]) for k in range(HARM)]
-    copies.append(pltpu.make_async_copy(var_vmem, var_ref, sems.at[HARM]))
+    copies = [pltpu.make_async_copy(var_vmem, var_ref, sems.at[4])]
+    for k in range(4):
+        rows = pl.ds(4 * k, 4)
+        copies.append(pltpu.make_async_copy(coef_vmem.at[rows], coef_ref.at[rows], sems.at[k]))
     for copy in copies:
         copy.start()
     for copy in copies:
@@ -554,7 +556,7 @@
         ),
         in_specs=[pl.BlockSpec(memory_space=pltpu.VMEM)] * 2,
         out_specs=(pl.BlockSpec(memory_space=pl.ANY), pl.BlockSpec(memory_space=pl.ANY)),
-        scratch_shapes=[pltpu.SemaphoreType.DMA((HARM + 1,))],
+        scratch_shapes=[pltpu.SemaphoreType.DMA((5,))],
         compiler_params=pltpu.CompilerParams(vmem_limit_bytes=4 * 1024 * 1024),
     )(coeffs, variance)
     return coeffs.reshape(HARM, 256, 128), variance.reshape(256, 128)

time: 114 us -> 114 us (level)
  no operation moved by 1% of the time
where the time goes in v8:
time: 114 us; the launch traced here: 113 us
  Pallas kernels  113 us (99%)
    pallas_call x1, Pallas kernels, local(): pl.pallas_call(functools.partial(kernel, fit, root), out_shape=(pltpu.VME...  111 us

profile of v8, /device:TPU:1, one launch (start us, length us, event | category | flops | bytes accessed | tf_op | source)
XLA Modules:
  0.0 113.5 jit_solution(2185306167835022958)
XLA Ops:
  0.6 111.5 %shard_map.41 = (f32[16,32,8,128]{3,2,1,0:T(8,128)S(1)}, f32[32,8,128]{2,1,0:T(8,128)S(1)}) custom-call(f32[384]{0:T(512)} %constant.2.clone.table_hbm, f32[3,16,4,4,2,2,8,128]{7,6,5,4,3,2,1,0:T(8,128)} %bitcast.7), custom_call_target="tpu_custom_call" | custom-call | tf_op jit(solution)/shard_map/pallas_call | solution.py:538
  112.1 1.4 %shard_map.42 = (f32[16,32,8,128]{3,2,1,0:T(8,128)}, f32[32,8,128]{2,1,0:T(8,128)}) custom-call(f32[16,32,8,128]{3,2,1,0:T(8,128)S(1)} %get-tuple-element.6.coef_vmem, f32[32,8,128]{2,1,0:T(8,128)S(1)} %get-tuple-element.7.var_vmem), custom_call_target="tpu_custom_call" | custom-call | tf_op jit(solution)/shard_map/pallas_call | solution.py:551
